TPU v7x, 8 devices: a whole 2x2x1 slice. The times are simulated.
8 devices in a mesh: tp: 4 (over z, y, x), dp: 2 (over core).
Axes of the slice: x: 2, y: 2, z: 1, core: 2. Of those that a mesh axis runs over, the one named last changes fastest.
Arguments:
- x: bfloat16 [4096, 8192], P(('dp', 'tp'))
- w_gate: bfloat16 [8192, 28672], P('dp', 'tp')
- w_up: bfloat16 [8192, 28672], P('dp', 'tp')
- w_down: bfloat16 [28672, 8192], P('tp', 'dp')
Outputs:
- output: bfloat16 [4096, 8192], P(('dp', 'tp'))
All inputs are finite; a program needn't handle non-finite values.
Results may differ from a plain program's by a relative error of at most 0.0131236.
Values are sent between devices in bfloat16 or wider.
A program may use at most 1 GiB of HBM per device.

v0:
```python
import jax
import jax.numpy as jnp
from jax import lax
from jax.sharding import PartitionSpec as P


def solution(mesh):
    nt = mesh.shape["tp"]
    nd = mesh.shape["dp"]

    def body(x, wg, wu, wd):
        r, d = x.shape
        dc = d // nd
        xt = lax.all_gather(x, "tp", axis=0, tiled=True)
        xc = lax.all_to_all(xt, "dp", 1, 0, tiled=True)
        pa = jnp.dot(xc, wg, preferred_element_type=jnp.float32).astype(jnp.bfloat16)
        pb = jnp.dot(xc, wu, preferred_element_type=jnp.float32).astype(jnp.bfloat16)
        a = lax.psum_scatter(pa, "dp", scatter_dimension=0, tiled=True).astype(jnp.float32)
        b = lax.psum_scatter(pb, "dp", scatter_dimension=0, tiled=True).astype(jnp.float32)
        h = (jax.nn.silu(a) * b).astype(jnp.bfloat16)
        hg = lax.all_gather(h, "dp", axis=0, tiled=True)
        po = jnp.dot(hg, wd, preferred_element_type=jnp.float32).astype(jnp.bfloat16)
        po = po.reshape(nd, nt, r, dc)
        ps = lax.psum_scatter(po, "tp", scatter_dimension=1, tiled=True)
        o = lax.all_to_all(ps.reshape(nd, r, dc), "dp", 0, 0, tiled=True)
        o = o.transpose(1, 0, 2).reshape(r, d)
        return (x.astype(jnp.float32) + o.astype(jnp.float32)).astype(jnp.bfloat16)

    return jax.shard_map(body, mesh=mesh, in_specs=(P(("dp", "tp"), None), P("dp", "tp"), P("dp", "tp"), P("tp", "dp")), out_specs=P(("dp", "tp"), None), check_vma=False)
```

profile of v0, /device:TPU:0, one launch (start us, length us, event | category | flops | bytes accessed | tf_op | source)
XLA Modules:
  0.0 1997.9 jit_solution(9847009886764509500)
XLA Ops:
  6.5 0.0 all-gather.3.cloned.1.call-start
  6.5 11.9 copy.12
  18.5 0.0 all-gather.3.cloned.1.call-update
  18.5 0.0 reduce-scatter.12.cloned.1.call-start
  18.5 294.3 %all-gather.3.cloned.1.call-done = bf16[2048,8192]{0,1:T(8,128)(2,1)} async-done(((bf16[512,8192]{0,1:T(8,128)(2,1)}), bf16[2048,8192]{0,1:T(8,128)(2,1)}) %all-gather.3.cloned.1.call-update) | async-done | bytes 33554448 | tf_op jit(solution)/shard_map/all_gather | solution.py:14
  312.8 57.8 %all_to_all.24 = bf16[2048,2,4096]{0,2,1:T(8,128)(2,1)} all-to-all(bf16[2048,2,4096]{0,2,1:T(8,128)(2,1)} %bitcast.29), channel_id=1, replica_groups=mesh['tp'=4,'dp'=2] {'dp'}, dimensions={1} | all-to-all | bytes 67108864 | tf_op jit(solution)/shard_map/all_to_all | solution.py:15
  370.6 40.6 %copy.14 = bf16[2,2048,4096]{2,1,0:T(8,128)(2,1)} copy(bf16[2,2048,4096]{1,2,0:T(8,128)(2,1)} %bitcast.25) | data formatting | bytes 67108864 | tf_op jit(solution)/shard_map/all_to_all | solution.py:15
  411.3 256.8 %convolution_convert_fusion.1 = bf16[4096,7168]{1,0:T(8,128)(2,1)} fusion(bf16[4096,4096]{1,0:T(8,128)(2,1)} %bitcast.27, bf16[4096,7168]{1,0:T(8,128)(2,1)} %param.5), kind=kOutput, calls=%fused_computation.8 | convolution fusion | flops 240547528704 | bytes 150994944 | tf_op jit(solution)/shard_map/dot_general | solution.py:16
  668.1 0.0 reduce-scatter.12.cloned.1.call-update
  668.1 0.2 reduce-scatter.14.cloned.1.call-start
  668.3 259.4 %convolution_convert_fusion = bf16[4096,7168]{1,0:T(8,128)(2,1)} fusion(bf16[4096,4096]{1,0:T(8,128)(2,1)} %bitcast.28, bf16[4096,7168]{1,0:T(8,128)(2,1)} %param.6), kind=kOutput, calls=%fused_computation.7 | convolution fusion | flops 240547528704 | bytes 150994944 | tf_op jit(solution)/shard_map/dot_general | solution.py:17
  927.7 0.0 reduce-scatter.14.cloned.1.call-update
  927.7 0.0 all-gather.5.cloned.1.call-start
  927.8 0.0 reduce-scatter.12.cloned.1.call-done
  927.8 73.5 %reduce-scatter.14.cloned.1.call-done = bf16[2048,7168]{1,0:T(8,128)(2,1)} async-done(((bf16[4096,7168]{1,0:T(8,128)(2,1)}), bf16[2048,7168]{1,0:T(8,128)(2,1)}) %reduce-scatter.14.cloned.1.call-update) | async-done | bytes 29360144
  1001.3 29.9 %fusion.4 = bf16[2048,7168]{1,0:T(8,128)(2,1)} fusion(bf16[2048,7168]{1,0:T(8,128)(2,1)} %reduce-scatter.14.cloned.1.call-done, bf16[2048,7168]{1,0:T(8,128)(2,1)} %reduce-scatter.12.cloned.1.call-done), kind=kLoop, calls=%fused_computation.6 | loop fusion | flops 117440512 | bytes 88080384 | tf_op jit(solution)/shard_map/convert_element_type | solution.py:20
  1031.2 0.0 all-gather.5.cloned.1.call-update
  1031.2 0.3 all-reduce.5.cloned.1.call-start
  1031.5 82.4 %all-gather.5.cloned.1.call-done = bf16[4096,7168]{1,0:T(8,128)(2,1)} async-done(((bf16[2048,7168]{1,0:T(8,128)(2,1)}), bf16[4096,7168]{1,0:T(8,128)(2,1)}) %all-gather.5.cloned.1.call-update) | async-done | bytes 58720272 | tf_op jit(solution)/shard_map/all_gather | solution.py:21
  1113.9 257.4 %convolution_convert_fusion.2 = bf16[4096,4096]{1,0:T(8,128)(2,1)} fusion(bf16[4096,7168]{1,0:T(8,128)(2,1)} %all-gather.5.cloned.1.call-done, bf16[7168,4096]{1,0:T(8,128)(2,1)} %param.7), kind=kOutput, calls=%fused_computation.9 | convolution fusion | flops 240534945792 | bytes 150994944 | tf_op jit(solution)/shard_map/dot_general | solution.py:22
  1371.2 0.0 copy-start
  1371.2 0.0 all-reduce.5.cloned.1.call-update
  1371.3 0.6 copy-done
  1371.9 0.6 dynamic-slice.4
  1372.5 566.6 %all-reduce.5.cloned.1.call-done = bf16[2,4,512,4096]{3,2,1,0:T(8,128)(2,1)} async-done(((bf16[2,4,512,4096]{3,2,1,0:T(8,128)(2,1)}), bf16[2,4,512,4096]{3,2,1,0:T(8,128)(2,1)}) %all-reduce.5.cloned.1.call-update) | async-done | bytes 33554448
  1939.2 8.4 constant_dynamic-slice_fusion
  1947.6 12.0 copy.15
  1959.5 12.1 all_to_all.25
  1971.6 7.9 fusion.5
  1979.5 11.9 copy.16
Async XLA Ops:
  6.5 306.3 %all-gather.3.cloned.1.call-start = ((), (), s32[]{:S(2)}) async-start(), calls=%async_computation.4 | async-start | bytes 41943040 | tf_op jit(solution)/shard_map/all_gather | solution.py:14
  18.5 909.3 %reduce-scatter.12.cloned.1.call-start = ((), (), s32[]{:S(2)}) async-start(), calls=%async_computation.7 | async-start | bytes 88080384
  668.1 333.2 %reduce-scatter.14.cloned.1.call-start = ((), (), s32[]{:S(2)}) async-start(), calls=%async_computation.8 | async-start | bytes 88080384
  927.7 186.2 %all-gather.5.cloned.1.call-start = ((), (), s32[]{:S(2)}) async-start(), calls=%async_computation.5 | async-start | bytes 88080384 | tf_op jit(solution)/shard_map/all_gather | solution.py:21
  1031.2 908.0 %all-reduce.5.cloned.1.call-start = ((), (), s32[]{:S(2)}) async-start(), calls=%async_computation.6 | async-start | bytes 67108864
  1371.2 0.7 copy-start
Sparse Core Ops, SparseCore 0:
  18.6 294.1 all-gather.2
  668.2 74.1 reduce-scatter.11
  927.8 73.3 reduce-scatter.13
  1031.3 82.4 all-gather.4
  1371.4 567.7 all-reduce.4
where the time goes:
time: 2000 us
  waiting for transfers between devices  1020 us (51%)
  matrix products  774 us (39%)
  local copies, waits for them, and re-layouts  86.1 us (4%)
  blocking collectives  69.9 us (3%)
  other arithmetic  37.8 us (2%)
    unnamed x8, waiting for transfers between devices  640 us
    all_gather x1, waiting for transfers between devices, body(): xt = lax.all_gather(x, 'tp', axis=0, tiled=True)  294 us
    dot_general x1, matrix products, body(): jnp.dot(xc, wu, preferred_element_type=jnp.float32).astype(jnp.bfloat16)  259 us
    dot_general x1, matrix products, body(): jnp.dot(hg, wd, preferred_element_type=jnp.float32).astype(jnp.bfloat16)  257 us
    dot_general x1, matrix products, body(): jnp.dot(xc, wg, preferred_element_type=jnp.float32).astype(jnp.bfloat16)  257 us
    all_gather x1, waiting for transfers between devices, body(): hg = lax.all_gather(h, 'dp', axis=0, tiled=True)  82.4 us
    all_to_all x1, blocking collectives, body(): xc = lax.all_to_all(xt, 'dp', 1, 0, tiled=True)  57.8 us
    all_to_all x1, local copies, waits for them, and re-layouts, body(): xc = lax.all_to_all(xt, 'dp', 1, 0, tiled=True)  40.6 us
  transfers between devices with their start and end apart: 5, of which 4 were waited for; matrix products, arithmetic and copies ran while one was open for 13% of the time, Pallas kernels for 0%

commit v1 on v0

v1 whole, which is shorter than its diff:
```python
import functools

import jax
import jax.numpy as jnp
from jax import lax
from jax.experimental import pallas as pl
from jax.experimental.pallas import tpu as pltpu
from jax.sharding import PartitionSpec as P


BF = jnp.bfloat16
F32 = jnp.float32
VMEM_BYTES = 67_000_000


def mm(a, b):
    return jnp.dot(a, b, preferred_element_type=F32)


def first_step(fn):
    pl.when(pl.program_id(0) == 0)(fn)


def up_tiles(base, x, w, xv, wv, xsem, wsem):
    i, n = pl.program_id(0), pl.num_programs(0)
    tn = wv.shape[-1]
    slot = lax.rem(i, 2)

    def w_copy(t, j):
        at, cols = lax.rem(t, 2), pl.ds(pl.multiple_of(base + t * tn, tn), tn)
        return pltpu.make_async_copy(w[j].at[:, cols], wv.at[at, j], wsem.at[at, j])

    def x_copy(c):
        return pltpu.make_async_copy(x[c], xv.at[c], xsem.at[c])

    @first_step
    def _():
        x_copy(0).start()
        w_copy(0, 0).start()

    w_copy(i, 0).wait()

    @first_step
    def _():
        x_copy(0).wait()
        w_copy(0, 1).start()
        x_copy(1).start()

    a = mm(xv[0], wv[slot, 0])
    w_copy(i, 1).wait()

    @pl.when(i + 1 < n)
    def _():
        w_copy(i + 1, 0).start()
        w_copy(i + 1, 1).start()

    yield 0, a, mm(xv[0], wv[slot, 1])

    @first_step
    def _():
        x_copy(1).wait()

    yield 1, mm(xv[1], wv[slot, 0]), mm(xv[1], wv[slot, 1])


def give_kernel(rows, half, start, off, x0, x1, wg, wu, pa, pb, *scratch):
    base = off[0] * half + start
    for c, a, b in up_tiles(base, (x0, x1), (wg, wu), *scratch):
        pa[pl.ds(c * rows, rows), :] = a.astype(BF)
        pb[pl.ds(c * rows, rows), :] = b.astype(BF)


def keep_kernel(rows, half, start, off, x0, x1, wg, wu, ra, rb, h, *scratch):
    base = off[0] * half + start
    for c, a, b in up_tiles(base, (x0, x1), (wg, wu), *scratch):
        theirs = pl.ds((1 - c) * rows, rows)
        a = a + ra[theirs, :].astype(F32)
        b = b + rb[theirs, :].astype(F32)
        h[pl.ds(c * rows, rows), :] = (jax.nn.silu(a) * b).astype(BF)


def down_kernel(rows, half, starts, chunks, n_add, off, *refs):
    n_h = len(starts)
    own, got, wd = refs[:n_h], refs[n_h : 2 * n_h], refs[2 * n_h]
    refs = refs[2 * n_h + 1 :]
    adds, outs = refs[:n_add], refs[n_add : n_add + len(chunks)]
    hv, wv, hsem, wsem = refs[-4:]
    i, n = pl.program_id(0), pl.num_programs(0)
    tn = wv.shape[-1]

    def w_copy(t):
        at, cols = lax.rem(t, 2), pl.ds(pl.multiple_of(t * tn, tn), tn)
        return pltpu.make_async_copy(wd.at[:, cols], wv.at[at], wsem.at[at])

    def h_copies(k):
        for j, start in enumerate(starts):
            for g, (src, c, side) in enumerate(((own[j], chunks[k], off[0]), (got[j], 1 - chunks[k], 1 - off[0]))):
                cols = pl.ds(pl.multiple_of(side * half + start, 128), src.shape[1])
                yield pltpu.make_async_copy(
                    src.at[pl.ds(c * rows, rows), :], hv.at[k, :, cols], hsem.at[k, j, g]
                )

    @first_step
    def _():
        for c in h_copies(0):
            c.start()
        w_copy(0).start()

    w_copy(i).wait()

    @first_step
    def _():
        for c in h_copies(0):
            c.wait()
        if len(chunks) > 1:
            for c in h_copies(1):
                c.start()

    @pl.when(i + 1 < n)
    def _():
        w_copy(i + 1).start()

    for k in range(len(chunks)):
        if k:

            @first_step
            def _():
                for c in h_copies(k):
                    c.wait()

        o = mm(hv[k], wv[lax.rem(i, 2)])
        if n_add:
            o = o + adds[k][...].astype(F32)
        outs[k][...] = o.astype(BF)


def finish_kernel(off, x, m0, m1, p0, p1, y):
    n = m0.shape[1]
    for at, lhs, rhs in ((off[0], m0, m1), (1 - off[0], p0, p1)):
        cols = pl.ds(pl.multiple_of(at * n, 128), n)
        o = lhs[...].astype(F32) + rhs[...].astype(F32)
        y[:, cols] = (x[:, cols].astype(F32) + o).astype(BF)


def solution(mesh):
    nt = mesh.shape["tp"]
    nd = mesh.shape["dp"]
    axes = ("tp", "dp")

    def pairs(bit0, bit1, flip):
        return [(t * nd + d, (t ^ (bit0, bit1)[d]) * nd + (d ^ flip)) for t in range(nt) for d in range(nd)]

    perms = {"a": pairs(1, 2, 0), "b": pairs(2, 1, 0), "c": pairs(0, 0, 1), "ax": pairs(1, 2, 1), "bx": pairs(2, 1, 1)}

    def body(x, wg, wu, wd):
        r, d = x.shape
        dc = d // nd
        f = wg.shape[1]
        half, tn = f // 2, 512
        tiles = half // tn
        cut = (tiles + 1) // 2
        whole, parts = ((0, tiles),), ((0, cut), (cut, tiles - cut))
        me = lax.axis_index("dp")
        mine, other = me.reshape(1), (1 - me).reshape(1)
        last = [None]
        anywhere = pl.BlockSpec(memory_space=pl.ANY)
        params = pltpu.CompilerParams(dimension_semantics=("arbitrary",), vmem_limit_bytes=VMEM_BYTES)

        def hop(v, kind):
            return lax.ppermute(v, axes, perms[kind])

        def after(v):
            if last[0] is None:
                return v
            return lax.optimization_barrier((v, last[0]))[0]

        def run(call, args):
            out = call(*args)
            last[0] = out[0] if isinstance(out, (list, tuple)) else out
            return out

        def up(kernel, who, span, xs, extra, n_out):
            start, count = span
            t_spec = pl.BlockSpec((2 * r, tn), lambda i, o: (0, i))
            width = count * tn
            call = pl.pallas_call(
                functools.partial(kernel, r, half, start * tn),
                grid_spec=pltpu.PrefetchScalarGridSpec(
                    num_scalar_prefetch=1,
                    grid=(count,),
                    in_specs=[anywhere] * 4 + [t_spec] * len(extra),
                    out_specs=[t_spec] * n_out,
                    scratch_shapes=[
                        pltpu.VMEM((2, r, dc), BF),
                        pltpu.VMEM((2, 2, dc, tn), BF),
                        pltpu.SemaphoreType.DMA((2,)),
                        pltpu.SemaphoreType.DMA((2, 2)),
                    ],
                ),
                out_shape=[jax.ShapeDtypeStruct((2 * r, width), BF)] * n_out,
                compiler_params=params,
                cost_estimate=pl.CostEstimate(
                    flops=8 * r * dc * width, bytes_accessed=4 * (r * dc + dc * width + r * width), transcendentals=0
                ),
            )
            return run(call, (who, after(xs[0]), xs[1], wg, wu, *extra))

        def give(xs, spans=whole, q=0):
            pa, pb = up(give_kernel, other, spans[q], xs, (), 2)
            return hop(pa, "c"), hop(pb, "c")

        def keep(xs, got, spans=whole, q=0):
            (h,) = up(keep_kernel, mine, spans[q], xs, got, 1)
            return h, hop(h, "c"), spans[q][0] * tn

        def down(hs, chunks, adds=()):
            own, got, starts = zip(*hs)
            n = len(chunks)
            o_spec = pl.BlockSpec((r, tn), lambda i, o: (0, i))
            call = pl.pallas_call(
                functools.partial(down_kernel, r, half, starts, chunks, len(adds)),
                grid_spec=pltpu.PrefetchScalarGridSpec(
                    num_scalar_prefetch=1,
                    grid=(dc // tn,),
                    in_specs=[anywhere] * (2 * len(hs) + 1) + [o_spec] * len(adds),
                    out_specs=[o_spec] * n,
                    scratch_shapes=[
                        pltpu.VMEM((n, r, f), BF),
                        pltpu.VMEM((2, f, tn), BF),
                        pltpu.SemaphoreType.DMA((n, len(hs), 2)),
                        pltpu.SemaphoreType.DMA((2,)),
                    ],
                ),
                out_shape=[jax.ShapeDtypeStruct((r, dc), BF)] * n,
                compiler_params=params,
                cost_estimate=pl.CostEstimate(
                    flops=2 * n * r * f * dc, bytes_accessed=2 * (n * r * f + f * dc + n * r * dc), transcendentals=0
                ),
            )
            return run(call, (mine, after(own[0]), *own[1:], *got, wd, *adds))

        xm = lax.dynamic_slice_in_dim(x, me * dc, dc, 1)
        xp = hop(lax.dynamic_slice_in_dim(x, (1 - me) * dc, dc, 1), "c")
        x1m = hop(xm, "a")
        x1p = hop(xp, "b")
        u0 = (xm, xp)
        g00 = give(u0, parts, 0)
        g01 = give(u0, parts, 1)
        k00 = keep(u0, g00, parts, 0)
        x2m, x2p = hop(x1m, "b"), hop(x1p, "a")
        k01 = keep(u0, g01, parts, 1)
        u1, u2 = (x1m, x1p), (x2m, x2p)
        g1 = give(u1)
        x3m, x3p = hop(xm, "b"), hop(xp, "a")
        u3 = (x3m, x3p)
        g2 = give(u2)
        k1 = keep(u1, g1)
        k2 = keep(u2, g2)
        g3 = give(u3)
        o2m, o2p = down((k2,), (0, 1))
        s2m, s2p = hop(o2m, "a"), hop(o2p, "b")
        o1m, o1p = down((k1,), (0, 1))
        y1m, y1p = hop(o1m, "a"), hop(o1p, "b")
        k3 = keep(u3, g3)
        (o3p,) = down((k3,), (1,), (s2p,))
        y3p = hop(o3p, "ax")
        (o3m,) = down((k3,), (0,), (s2m,))
        y3m = hop(o3m, "b")
        (op,) = down((k00, k01), (1,), (y1p,))
        rp = hop(op, "c")
        (om,) = down((k00, k01), (0,), (y1m,))
        rows = min(r, 64)
        half = pl.BlockSpec((rows, dc), lambda i, o: (i, 0))
        full = pl.BlockSpec((rows, d), lambda i, o: (i, 0))
        call = pl.pallas_call(
            finish_kernel,
            grid_spec=pltpu.PrefetchScalarGridSpec(
                num_scalar_prefetch=1, grid=(r // rows,), in_specs=[full] + [half] * 4, out_specs=full
            ),
            out_shape=jax.ShapeDtypeStruct((r, d), BF),
            compiler_params=pltpu.CompilerParams(dimension_semantics=("arbitrary",)),
            cost_estimate=pl.CostEstimate(flops=3 * r * d, bytes_accessed=8 * r * d, transcendentals=0),
            name="finish",
        )
        return run(call, (mine, x, om, y3m, rp, y3p))

    return jax.shard_map(body, mesh=mesh, in_specs=(P(("dp", "tp"), None), P("dp", "tp"), P("dp", "tp"), P("tp", "dp")), out_specs=P(("dp", "tp"), None), check_vma=False)
```

time: 2000 us -> 1090 us (0.55)
  Pallas kernels: 0 us -> 900 us
  waiting for transfers between devices: 1020 us -> 160 us
  matrix products: 774 us -> 0 us
  local copies, waits for them, and re-layouts: 86.1 us -> 6.29 us
  blocking collectives: 69.9 us -> 0 us
  other arithmetic: 37.8 us -> 0 us
    pallas_call x0 -> x17, Pallas kernels: none -> 900 us  [run(): out = call(*args)]
    dot_general x3 -> x0, matrix products: 774 us -> none  [the longest x1 259 us: body(): jnp.dot(xc, wu, preferred_element_type=jnp.float32).astype(jnp.bfloat16)]
    unnamed x8 -> x0, waiting for transfers between devices: 640 us -> none
    all_gather x2 -> x0, waiting for transfers between devices: 377 us -> none  [the longest x1 294 us: body(): xt = lax.all_gather(x, 'tp', axis=0, tiled=True)]
    ppermute x0 -> x29, waiting for transfers between devices: none -> 160 us  [hop(): return lax.ppermute(v, axes, perms[kind])]
    all_to_all x2 -> x0, blocking collectives: 69.9 us -> none  [the longest x1 57.8 us: body(): xc = lax.all_to_all(xt, 'dp', 1, 0, tiled=True)]
    all_to_all x1 -> x0, local copies, waits for them, and re-layouts: 40.6 us -> none  [body(): xc = lax.all_to_all(xt, 'dp', 1, 0, tiled=True)]
    convert_element_type x2 -> x0, other arithmetic: 37.8 us -> none  [the longest x1 29.9 us: body(): h = (jax.nn.silu(a) * b).astype(jnp.bfloat16)]
  transfers between devices with their start and end apart: 5 -> 29, of which waited for: 4 -> 5; matrix products, arithmetic and copies ran while one was open for 13% -> 0% of each run, Pallas kernels for 0% -> 75%
where the time goes in v1:
time: 1090 us
  Pallas kernels  900 us (83%)
  waiting for transfers between devices  160 us (15%)
  starting transfers between devices  20.1 us (2%)
    pallas_call x17, Pallas kernels, run(): out = call(*args)  900 us
    ppermute x29, waiting for transfers between devices, hop(): return lax.ppermute(v, axes, perms[kind])  160 us
  transfers between devices with their start and end apart: 29, of which 5 were waited for; matrix products, arithmetic and copies ran while one was open for 0% of the time, Pallas kernels for 75%

profile of v1, /device:TPU:0, one launch (start us, length us, event | category | flops | bytes accessed | tf_op | source)
XLA Modules:
  0.0 1086.8 jit_solution(16466424187330556787)
XLA Ops:
  0.0 6.3 constant_dynamic-slice_fusion
  6.3 0.8 collective-permute-start
  7.1 2.5 collective-permute-start.4
  9.6 4.4 collective-permute-done.x1
  14.0 41.3 %shard_map.46 = (bf16[1024,2048]{1,0:T(8,128)(2,1)}, bf16[1024,2048]{1,0:T(8,128)(2,1)}) custom-call(s32[1]{0:T(128)} %bitcast.1.off, bf16[512,4096]{1,0:T(8,128)(2,1)} %get-tuple-element.39.x0, bf16[512,4096]{1,0:T(8,128)(2,1)} %collective-permute-done.x1, bf16[4096,7168]{1,0:T(8,128)(2,1)} %wg.19, bf16[4096,7168]{1,0:T(8,128)(2,1)} %wu.19), custom_call_target="tpu_custom_call" | custom-call | flops 34359738368 | bytes 46137344 | tf_op jit(solution)/shard_map/pallas_call | solution.py:178
  55.4 0.4 collective-permute-start.1
  55.8 0.1 collective-permute-start.2
  55.9 32.2 %shard_map.47 = (bf16[1024,1536]{1,0:T(8,128)(2,1)}, bf16[1024,1536]{1,0:T(8,128)(2,1)}) custom-call(s32[1]{0:T(128)} %bitcast.1.off, bf16[512,4096]{1,0:T(8,128)(2,1)} %get-tuple-element.39.x0, bf16[512,4096]{1,0:T(8,128)(2,1)} %collective-permute-done.x1, bf16[4096,7168]{1,0:T(8,128)(2,1)} %wg.19, bf16[4096,7168]{1,0:T(8,128)(2,1)} %wu.19), custom_call_target="tpu_custom_call" | custom-call | flops 25769803776 | bytes 36700160 | tf_op jit(solution)/shard_map/pallas_call | solution.py:178
  88.0 0.4 collective-permute-start.6
  88.5 0.1 collective-permute-start.7
  88.6 0.0 collective-permute-done.4.x0
  88.6 2.9 collective-permute-start.8
  91.5 0.0 collective-permute-start.5
  91.5 0.0 collective-permute-done.2.rb
  91.5 46.6 %shard_map.48.refs_0_ = bf16[1024,2048]{1,0:T(8,128)(2,1)} custom-call(s32[1]{0:T(128)} %bitcast.off, bf16[512,4096]{1,0:T(8,128)(2,1)} %get-tuple-element.39.x0, bf16[512,4096]{1,0:T(8,128)(2,1)} %collective-permute-done.x1, bf16[4096,7168]{1,0:T(8,128)(2,1)} %wg.19, bf16[4096,7168]{1,0:T(8,128)(2,1)} %wu.19, bf16[1024,2048]{1,0:T(8,128)(2,1)} %collective-permute-done.1.ra, ...), custom_call_target="tpu_custom_call" | custom-call | flops 34359738368 | bytes 46137344 | tf_op jit(solution)/shard_map/pallas_call | solution.py:178
  138.1 0.0 collective-permute-done.7.rb
  138.1 36.6 %shard_map.49.refs_1_ = bf16[1024,1536]{1,0:T(8,128)(2,1)} custom-call(s32[1]{0:T(128)} %bitcast.off, bf16[512,4096]{1,0:T(8,128)(2,1)} %get-tuple-element.39.x0, bf16[512,4096]{1,0:T(8,128)(2,1)} %collective-permute-done.x1, bf16[4096,7168]{1,0:T(8,128)(2,1)} %wg.19, bf16[4096,7168]{1,0:T(8,128)(2,1)} %wu.19, bf16[1024,1536]{1,0:T(8,128)(2,1)} %collective-permute-done.6.ra, ...), custom_call_target="tpu_custom_call" | custom-call | flops 25769803776 | bytes 36700160 | tf_op jit(solution)/shard_map/pallas_call | solution.py:178
  174.7 0.0 collective-permute-done.8.x1
  174.7 2.0 collective-permute-start.9
  176.7 69.1 %shard_map.50 = (bf16[1024,3584]{1,0:T(8,128)(2,1)}, bf16[1024,3584]{1,0:T(8,128)(2,1)}) custom-call(s32[1]{0:T(128)} %bitcast.1.off, bf16[512,4096]{1,0:T(8,128)(2,1)} %collective-permute-done.4.x0, bf16[512,4096]{1,0:T(8,128)(2,1)} %collective-permute-done.8.x1, bf16[4096,7168]{1,0:T(8,128)(2,1)} %wg.19, bf16[4096,7168]{1,0:T(8,128)(2,1)} %wu.19), custom_call_target="tpu_custom_call" | custom-call | flops 60129542144 | bytes 74448896 | tf_op jit(solution)/shard_map/pallas_call | solution.py:178
  245.9 0.0 collective-permute-start.10
  245.9 0.0 collective-permute-done.5.x0
  245.9 0.5 collective-permute-start.11
  246.4 0.0 collective-permute-done.9.x1
  246.4 68.9 %shard_map.51 = (bf16[1024,3584]{1,0:T(8,128)(2,1)}, bf16[1024,3584]{1,0:T(8,128)(2,1)}) custom-call(s32[1]{0:T(128)} %bitcast.1.off, bf16[512,4096]{1,0:T(8,128)(2,1)} %collective-permute-done.5.x0, bf16[512,4096]{1,0:T(8,128)(2,1)} %collective-permute-done.9.x1, bf16[4096,7168]{1,0:T(8,128)(2,1)} %wg.19, bf16[4096,7168]{1,0:T(8,128)(2,1)} %wu.19), custom_call_target="tpu_custom_call" | custom-call | flops 60129542144 | bytes 74448896 | tf_op jit(solution)/shard_map/pallas_call | solution.py:178
  315.3 0.1 collective-permute-start.12
  315.4 0.5 collective-permute-start.13
  315.9 1.5 collective-permute-start.3
  317.4 0.5 collective-permute-start.14
  317.9 75.1 %shard_map.52.refs_0_ = bf16[1024,3584]{1,0:T(8,128)(2,1)} custom-call(s32[1]{0:T(128)} %bitcast.off, bf16[512,4096]{1,0:T(8,128)(2,1)} %collective-permute-done.4.x0, bf16[512,4096]{1,0:T(8,128)(2,1)} %collective-permute-done.8.x1, bf16[4096,7168]{1,0:T(8,128)(2,1)} %wg.19, bf16[4096,7168]{1,0:T(8,128)(2,1)} %wu.19, ...), custom_call_target="tpu_custom_call" | custom-call | flops 60129542144 | bytes 74448896 | tf_op jit(solution)/shard_map/pallas_call | solution.py:178
  393.0 0.0 collective-permute-done.12.ra
  393.1 75.0 %shard_map.53.refs_0_ = bf16[1024,3584]{1,0:T(8,128)(2,1)} custom-call(s32[1]{0:T(128)} %bitcast.off, bf16[512,4096]{1,0:T(8,128)(2,1)} %collective-permute-done.5.x0, bf16[512,4096]{1,0:T(8,128)(2,1)} %collective-permute-done.9.x1, bf16[4096,7168]{1,0:T(8,128)(2,1)} %wg.19, bf16[4096,7168]{1,0:T(8,128)(2,1)} %wu.19, ...), custom_call_target="tpu_custom_call" | custom-call | flops 60129542144 | bytes 74448896 | tf_op jit(solution)/shard_map/pallas_call | solution.py:178
  468.1 0.0 collective-permute-start.15
  468.1 0.5 collective-permute-start.16
  468.6 69.3 %shard_map.54 = (bf16[1024,3584]{1,0:T(8,128)(2,1)}, bf16[1024,3584]{1,0:T(8,128)(2,1)}) custom-call(s32[1]{0:T(128)} %bitcast.1.off, bf16[512,4096]{1,0:T(8,128)(2,1)} %collective-permute-done.3.x0, bf16[512,4096]{1,0:T(8,128)(2,1)} %collective-permute-done.14.x1, bf16[4096,7168]{1,0:T(8,128)(2,1)} %wg.19, bf16[4096,7168]{1,0:T(8,128)(2,1)} %wu.19), custom_call_target="tpu_custom_call" | custom-call | flops 60129542144 | bytes 74448896 | tf_op jit(solution)/shard_map/pallas_call | solution.py:178
  537.9 0.1 collective-permute-start.17
  538.0 0.5 collective-permute-start.18
  538.4 70.7 %shard_map.55 = (bf16[512,4096]{1,0:T(8,128)(2,1)}, bf16[512,4096]{1,0:T(8,128)(2,1)}) custom-call(s32[1]{0:T(128)} %bitcast.off, bf16[1024,3584]{1,0:T(8,128)(2,1)} %shard_map.53.refs_0_, bf16[1024,3584]{1,0:T(8,128)(2,1)} %collective-permute-done.15.refs_1_, bf16[7168,4096]{1,0:T(8,128)(2,1)} %refs_4_.3), custom_call_target="tpu_custom_call" | custom-call | flops 60129542144 | bytes 81788928 | tf_op jit(solution)/shard_map/pallas_call | solution.py:178
  609.1 0.0 collective-permute-done.16.refs_1_
  609.1 70.9 %shard_map.56 = (bf16[512,4096]{1,0:T(8,128)(2,1)}, bf16[512,4096]{1,0:T(8,128)(2,1)}) custom-call(s32[1]{0:T(128)} %bitcast.off, bf16[1024,3584]{1,0:T(8,128)(2,1)} %shard_map.52.refs_0_, bf16[1024,3584]{1,0:T(8,128)(2,1)} %collective-permute-done.16.refs_1_, bf16[7168,4096]{1,0:T(8,128)(2,1)} %refs_4_.3), custom_call_target="tpu_custom_call" | custom-call | flops 60129542144 | bytes 81788928 | tf_op jit(solution)/shard_map/pallas_call | solution.py:178
  680.0 0.0 collective-permute-done.17.ra
  680.0 74.9 %shard_map.57.refs_0_ = bf16[1024,3584]{1,0:T(8,128)(2,1)} custom-call(s32[1]{0:T(128)} %bitcast.off, bf16[512,4096]{1,0:T(8,128)(2,1)} %collective-permute-done.3.x0, bf16[512,4096]{1,0:T(8,128)(2,1)} %collective-permute-done.14.x1, bf16[4096,7168]{1,0:T(8,128)(2,1)} %wg.19, bf16[4096,7168]{1,0:T(8,128)(2,1)} %wu.19, ...), custom_call_target="tpu_custom_call" | custom-call | flops 60129542144 | bytes 74448896 | tf_op jit(solution)/shard_map/pallas_call | solution.py:178
  755.0 0.1 collective-permute-start.19
  755.1 0.4 collective-permute-start.20
  755.5 1.6 collective-permute-start.21
  757.1 0.5 collective-permute-start.22
  757.6 90.6 %collective-permute-done.20.refs_3_ = bf16[512,4096]{1,0:T(8,128)(2,1)} collective-permute-done((bf16[512,4096]{1,0:T(8,128)(2,1)}, bf16[512,4096]{1,0:T(8,128)(2,1)}, u32[]{:S(2)}, u32[]{:S(2)}) %collective-permute-start.20) | collective-permute-done | bytes 4194336 | tf_op jit(solution)/shard_map/ppermute | solution.py:170
  848.2 1.8 collective-permute-start.25
  850.0 0.0 collective-permute-done.19.refs_1_
  850.0 0.4 collective-permute-start.24
  850.4 38.9 %shard_map.58 = bf16[512,4096]{1,0:T(8,128)(2,1)} custom-call(s32[1]{0:T(128)} %bitcast.off, bf16[1024,3584]{1,0:T(8,128)(2,1)} %shard_map.57.refs_0_, bf16[1024,3584]{1,0:T(8,128)(2,1)} %collective-permute-done.19.refs_1_, bf16[7168,4096]{1,0:T(8,128)(2,1)} %refs_4_.3, bf16[512,4096]{1,0:T(8,128)(2,1)} %collective-permute-done.20.refs_3_), custom_call_target="tpu_custom_call" | custom-call | flops 30064771072 | bytes 70254592 | tf_op jit(solution)/shard_map/pallas_call | solution.py:178
  889.4 39.2 %shard_map.59 = bf16[512,4096]{1,0:T(8,128)(2,1)} custom-call(s32[1]{0:T(128)} %bitcast.off, bf16[1024,3584]{1,0:T(8,128)(2,1)} %shard_map.57.refs_0_, bf16[1024,3584]{1,0:T(8,128)(2,1)} %collective-permute-done.19.refs_1_, bf16[7168,4096]{1,0:T(8,128)(2,1)} %refs_4_.3, bf16[512,4096]{1,0:T(8,128)(2,1)} %collective-permute-done.21.refs_3_), custom_call_target="tpu_custom_call" | custom-call | flops 30064771072 | bytes 70254592 | tf_op jit(solution)/shard_map/pallas_call | solution.py:178
  928.6 0.0 collective-permute-done.22.refs_2_
  928.6 11.7 %collective-permute-done.24.refs_5_ = bf16[512,4096]{1,0:T(8,128)(2,1)} collective-permute-done((bf16[512,4096]{1,0:T(8,128)(2,1)}, bf16[512,4096]{1,0:T(8,128)(2,1)}, u32[]{:S(2)}, u32[]{:S(2)}) %collective-permute-start.24) | collective-permute-done | bytes 4194336 | tf_op jit(solution)/shard_map/ppermute | solution.py:170
  940.3 39.0 %shard_map.60 = bf16[512,4096]{1,0:T(8,128)(2,1)} custom-call(s32[1]{0:T(128)} %bitcast.off, bf16[1024,2048]{1,0:T(8,128)(2,1)} %shard_map.48.refs_0_, bf16[1024,1536]{1,0:T(8,128)(2,1)} %shard_map.49.refs_1_, bf16[1024,2048]{1,0:T(8,128)(2,1)} %collective-permute-done.22.refs_2_, bf16[1024,1536]{1,0:T(8,128)(2,1)} %collective-permute-done.23.refs_3_, ...), custom_call_target="tpu_custom_call" | custom-call | flops 30064771072 | bytes 70254592 | tf_op jit(solution)/shard_map/pallas_call | solution.py:178
  979.3 0.0 collective-permute-start.27
  979.4 1.7 collective-permute-start.26
  981.0 0.2 collective-permute-start.28
  981.2 0.0 collective-permute-done.25.refs_5_
  981.2 39.1 %shard_map.61.m0 = bf16[512,4096]{1,0:T(8,128)(2,1)} custom-call(s32[1]{0:T(128)} %bitcast.off, bf16[1024,2048]{1,0:T(8,128)(2,1)} %shard_map.48.refs_0_, bf16[1024,1536]{1,0:T(8,128)(2,1)} %shard_map.49.refs_1_, bf16[1024,2048]{1,0:T(8,128)(2,1)} %collective-permute-done.22.refs_2_, bf16[1024,1536]{1,0:T(8,128)(2,1)} %collective-permute-done.23.refs_3_, ...), custom_call_target="tpu_custom_call" | custom-call | flops 30064771072 | bytes 70254592 | tf_op jit(solution)/shard_map/pallas_call | solution.py:178
  1020.3 0.0 collective-permute-done.27.p0
  1020.3 51.8 %collective-permute-done.26.m1 = bf16[512,4096]{1,0:T(8,128)(2,1)} collective-permute-done((bf16[512,4096]{1,0:T(8,128)(2,1)}, bf16[512,4096]{1,0:T(8,128)(2,1)}, u32[]{:S(2)}, u32[]{:S(2)}) %collective-permute-start.26) | collective-permute-done | bytes 4194336 | tf_op jit(solution)/shard_map/ppermute | solution.py:170
  1072.1 1.0 collective-permute-done.28.p1
  1073.1 13.4 %finish.1 = bf16[512,8192]{1,0:T(8,128)(2,1)} custom-call(s32[1]{0:T(128)} %bitcast.off, bf16[512,8192]{1,0:T(8,128)(2,1)} %x.1, bf16[512,4096]{1,0:T(8,128)(2,1)} %shard_map.61.m0, bf16[512,4096]{1,0:T(8,128)(2,1)} %collective-permute-done.26.m1, bf16[512,4096]{1,0:T(8,128)(2,1)} %collective-permute-done.27.p0, bf16[512,4096]{1,0:T(8,128)(2,1)} %collective-permute-done.28.p1), custom_call_target="tpu_custom_call" | custom-call | flops 12582912 | bytes 33554432 | tf_op jit(solution)/shard_map/finish/pallas_call | solution.py:178
  (12 shorter events, 0.0 us)
Async XLA Ops:
  6.3 7.8 collective-permute-start
  7.1 81.5 %collective-permute-start.4 = (bf16[512,4096]{1,0:T(8,128)(2,1)}, bf16[512,4096]{1,0:T(8,128)(2,1)}, u32[]{:S(2)}, u32[]{:S(2)}) collective-permute-start(bf16[512,4096]{1,0:T(8,128)(2,1)} %get-tuple-element.39.x0), channel_id=1, source_target_pairs={{0,2},{1,5},{2,0},{3,7},{4,6},{5,1},{6,4},{7,3}} | collective-permute-start | bytes 12582920 | tf_op jit(solution)/shard_map/ppermute | solution.py:170
  55.4 36.1 %collective-permute-start.1 = (bf16[1024,2048]{1,0:T(8,128)(2,1)}, bf16[1024,2048]{1,0:T(8,128)(2,1)}, u32[]{:S(2)}, u32[]{:S(2)}) collective-permute-start(bf16[1024,2048]{1,0:T(8,128)(2,1)} %get-tuple-element.34), channel_id=1, source_target_pairs={{0,1},{1,0},{2,3},{3,2},{4,5},{5,4},{6,7},{7,6}} | collective-permute-start | bytes 12582920 | tf_op jit(solution)/shard_map/ppermute | solution.py:170
  55.8 35.7 %collective-permute-start.2 = (bf16[1024,2048]{1,0:T(8,128)(2,1)}, bf16[1024,2048]{1,0:T(8,128)(2,1)}, u32[]{:S(2)}, u32[]{:S(2)}) collective-permute-start(bf16[1024,2048]{1,0:T(8,128)(2,1)} %get-tuple-element.38), channel_id=1, source_target_pairs={{0,1},{1,0},{2,3},{3,2},{4,5},{5,4},{6,7},{7,6}} | collective-permute-start | bytes 12582920 | tf_op jit(solution)/shard_map/ppermute | solution.py:170
  88.0 50.1 %collective-permute-start.6 = (bf16[1024,1536]{1,0:T(8,128)(2,1)}, bf16[1024,1536]{1,0:T(8,128)(2,1)}, u32[]{:S(2)}, u32[]{:S(2)}) collective-permute-start(bf16[1024,1536]{1,0:T(8,128)(2,1)} %get-tuple-element.36), channel_id=1, source_target_pairs={{0,1},{1,0},{2,3},{3,2},{4,5},{5,4},{6,7},{7,6}} | collective-permute-start | bytes 9437192 | tf_op jit(solution)/shard_map/ppermute | solution.py:170
  88.5 49.7 %collective-permute-start.7 = (bf16[1024,1536]{1,0:T(8,128)(2,1)}, bf16[1024,1536]{1,0:T(8,128)(2,1)}, u32[]{:S(2)}, u32[]{:S(2)}) collective-permute-start(bf16[1024,1536]{1,0:T(8,128)(2,1)} %get-tuple-element.40), channel_id=1, source_target_pairs={{0,1},{1,0},{2,3},{3,2},{4,5},{5,4},{6,7},{7,6}} | collective-permute-start | bytes 9437192 | tf_op jit(solution)/shard_map/ppermute | solution.py:170
  88.6 86.2 %collective-permute-start.8 = (bf16[512,4096]{1,0:T(8,128)(2,1)}, bf16[512,4096]{1,0:T(8,128)(2,1)}, u32[]{:S(2)}, u32[]{:S(2)}) collective-permute-start(bf16[512,4096]{1,0:T(8,128)(2,1)} %collective-permute-done.x1), channel_id=1, source_target_pairs={{0,4},{1,3},{2,6},{3,1},{4,0},{5,7},{6,2},{7,5}} | collective-permute-start | bytes 12582920 | tf_op jit(solution)/shard_map/ppermute | solution.py:170
  91.5 154.5 %collective-permute-start.5 = (bf16[512,4096]{1,0:T(8,128)(2,1)}, bf16[512,4096]{1,0:T(8,128)(2,1)}, u32[]{:S(2)}, u32[]{:S(2)}) collective-permute-start(bf16[512,4096]{1,0:T(8,128)(2,1)} %collective-permute-done.4.x0), channel_id=1, source_target_pairs={{0,4},{1,3},{2,6},{3,1},{4,0},{5,7},{6,2},{7,5}} | collective-permute-start | bytes 12582920 | tf_op jit(solution)/shard_map/ppermute | solution.py:170
  174.7 71.7 %collective-permute-start.9 = (bf16[512,4096]{1,0:T(8,128)(2,1)}, bf16[512,4096]{1,0:T(8,128)(2,1)}, u32[]{:S(2)}, u32[]{:S(2)}) collective-permute-start(bf16[512,4096]{1,0:T(8,128)(2,1)} %collective-permute-done.8.x1), channel_id=1, source_target_pairs={{0,2},{1,5},{2,0},{3,7},{4,6},{5,1},{6,4},{7,3}} | collective-permute-start | bytes 12582920 | tf_op jit(solution)/shard_map/ppermute | solution.py:170
  245.9 71.5 %collective-permute-start.10 = (bf16[1024,3584]{1,0:T(8,128)(2,1)}, bf16[1024,3584]{1,0:T(8,128)(2,1)}, u32[]{:S(2)}, u32[]{:S(2)}) collective-permute-start(bf16[1024,3584]{1,0:T(8,128)(2,1)} %get-tuple-element.42), channel_id=1, source_target_pairs={{0,1},{1,0},{2,3},{3,2},{4,5},{5,4},{6,7},{7,6}} | collective-permute-start | bytes 22020104 | tf_op jit(solution)/shard_map/ppermute | solution.py:170
  245.9 72.0 %collective-permute-start.11 = (bf16[1024,3584]{1,0:T(8,128)(2,1)}, bf16[1024,3584]{1,0:T(8,128)(2,1)}, u32[]{:S(2)}, u32[]{:S(2)}) collective-permute-start(bf16[1024,3584]{1,0:T(8,128)(2,1)} %get-tuple-element.46), channel_id=1, source_target_pairs={{0,1},{1,0},{2,3},{3,2},{4,5},{5,4},{6,7},{7,6}} | collective-permute-start | bytes 22020104 | tf_op jit(solution)/shard_map/ppermute | solution.py:170
  315.3 77.7 %collective-permute-start.12 = (bf16[1024,3584]{1,0:T(8,128)(2,1)}, bf16[1024,3584]{1,0:T(8,128)(2,1)}, u32[]{:S(2)}, u32[]{:S(2)}) collective-permute-start(bf16[1024,3584]{1,0:T(8,128)(2,1)} %get-tuple-element.44), channel_id=1, source_target_pairs={{0,1},{1,0},{2,3},{3,2},{4,5},{5,4},{6,7},{7,6}} | collective-permute-start | bytes 22020104 | tf_op jit(solution)/shard_map/ppermute | solution.py:170
  315.4 77.7 %collective-permute-start.13 = (bf16[1024,3584]{1,0:T(8,128)(2,1)}, bf16[1024,3584]{1,0:T(8,128)(2,1)}, u32[]{:S(2)}, u32[]{:S(2)}) collective-permute-start(bf16[1024,3584]{1,0:T(8,128)(2,1)} %get-tuple-element.48), channel_id=1, source_target_pairs={{0,1},{1,0},{2,3},{3,2},{4,5},{5,4},{6,7},{7,6}} | collective-permute-start | bytes 22020104 | tf_op jit(solution)/shard_map/ppermute | solution.py:170
  315.9 152.7 %collective-permute-start.3 = (bf16[512,4096]{1,0:T(8,128)(2,1)}, bf16[512,4096]{1,0:T(8,128)(2,1)}, u32[]{:S(2)}, u32[]{:S(2)}) collective-permute-start(bf16[512,4096]{1,0:T(8,128)(2,1)} %get-tuple-element.39.x0), channel_id=1, source_target_pairs={{0,4},{1,3},{2,6},{3,1},{4,0},{5,7},{6,2},{7,5}} | collective-permute-start | bytes 12582920 | tf_op jit(solution)/shard_map/ppermute | solution.py:170
  317.4 151.2 %collective-permute-start.14 = (bf16[512,4096]{1,0:T(8,128)(2,1)}, bf16[512,4096]{1,0:T(8,128)(2,1)}, u32[]{:S(2)}, u32[]{:S(2)}) collective-permute-start(bf16[512,4096]{1,0:T(8,128)(2,1)} %collective-permute-done.x1), channel_id=1, source_target_pairs={{0,2},{1,5},{2,0},{3,7},{4,6},{5,1},{6,4},{7,3}} | collective-permute-start | bytes 12582920 | tf_op jit(solution)/shard_map/ppermute | solution.py:170
  468.1 70.4 %collective-permute-start.15 = (bf16[1024,3584]{1,0:T(8,128)(2,1)}, bf16[1024,3584]{1,0:T(8,128)(2,1)}, u32[]{:S(2)}, u32[]{:S(2)}) collective-permute-start(bf16[1024,3584]{1,0:T(8,128)(2,1)} %shard_map.53.refs_0_), channel_id=1, source_target_pairs={{0,1},{1,0},{2,3},{3,2},{4,5},{5,4},{6,7},{7,6}} | collective-permute-start | bytes 22020104 | tf_op jit(solution)/shard_map/ppermute | solution.py:170
  468.1 141.0 %collective-permute-start.16 = (bf16[1024,3584]{1,0:T(8,128)(2,1)}, bf16[1024,3584]{1,0:T(8,128)(2,1)}, u32[]{:S(2)}, u32[]{:S(2)}) collective-permute-start(bf16[1024,3584]{1,0:T(8,128)(2,1)} %shard_map.52.refs_0_), channel_id=1, source_target_pairs={{0,1},{1,0},{2,3},{3,2},{4,5},{5,4},{6,7},{7,6}} | collective-permute-start | bytes 22020104 | tf_op jit(solution)/shard_map/ppermute | solution.py:170
  537.9 142.1 %collective-permute-start.17 = (bf16[1024,3584]{1,0:T(8,128)(2,1)}, bf16[1024,3584]{1,0:T(8,128)(2,1)}, u32[]{:S(2)}, u32[]{:S(2)}) collective-permute-start(bf16[1024,3584]{1,0:T(8,128)(2,1)} %get-tuple-element.50), channel_id=1, source_target_pairs={{0,1},{1,0},{2,3},{3,2},{4,5},{5,4},{6,7},{7,6}} | collective-permute-start | bytes 22020104 | tf_op jit(solution)/shard_map/ppermute | solution.py:170
  538.0 142.1 %collective-permute-start.18 = (bf16[1024,3584]{1,0:T(8,128)(2,1)}, bf16[1024,3584]{1,0:T(8,128)(2,1)}, u32[]{:S(2)}, u32[]{:S(2)}) collective-permute-start(bf16[1024,3584]{1,0:T(8,128)(2,1)} %get-tuple-element.56), channel_id=1, source_target_pairs={{0,1},{1,0},{2,3},{3,2},{4,5},{5,4},{6,7},{7,6}} | collective-permute-start | bytes 22020104 | tf_op jit(solution)/shard_map/ppermute | solution.py:170
  755.0 95.1 %collective-permute-start.19 = (bf16[1024,3584]{1,0:T(8,128)(2,1)}, bf16[1024,3584]{1,0:T(8,128)(2,1)}, u32[]{:S(2)}, u32[]{:S(2)}) collective-permute-start(bf16[1024,3584]{1,0:T(8,128)(2,1)} %shard_map.57.refs_0_), channel_id=1, source_target_pairs={{0,1},{1,0},{2,3},{3,2},{4,5},{5,4},{6,7},{7,6}} | collective-permute-start | bytes 22020104 | tf_op jit(solution)/shard_map/ppermute | solution.py:170
  755.1 93.1 %collective-permute-start.20 = (bf16[512,4096]{1,0:T(8,128)(2,1)}, bf16[512,4096]{1,0:T(8,128)(2,1)}, u32[]{:S(2)}, u32[]{:S(2)}) collective-permute-start(bf16[512,4096]{1,0:T(8,128)(2,1)} %get-tuple-element.58), channel_id=1, source_target_pairs={{0,4},{1,3},{2,6},{3,1},{4,0},{5,7},{6,2},{7,5}} | collective-permute-start | bytes 12582920 | tf_op jit(solution)/shard_map/ppermute | solution.py:170
  755.5 133.9 %collective-permute-start.21 = (bf16[512,4096]{1,0:T(8,128)(2,1)}, bf16[512,4096]{1,0:T(8,128)(2,1)}, u32[]{:S(2)}, u32[]{:S(2)}) collective-permute-start(bf16[512,4096]{1,0:T(8,128)(2,1)} %get-tuple-element.52), channel_id=1, source_target_pairs={{0,2},{1,5},{2,0},{3,7},{4,6},{5,1},{6,4},{7,3}} | collective-permute-start | bytes 12582920 | tf_op jit(solution)/shard_map/ppermute | solution.py:170
  757.1 171.5 %collective-permute-start.23 = (bf16[1024,1536]{1,0:T(8,128)(2,1)}, bf16[1024,1536]{1,0:T(8,128)(2,1)}, u32[]{:S(2)}, u32[]{:S(2)}) collective-permute-start(bf16[1024,1536]{1,0:T(8,128)(2,1)} %shard_map.49.refs_1_), channel_id=1, source_target_pairs={{0,1},{1,0},{2,3},{3,2},{4,5},{5,4},{6,7},{7,6}} | collective-permute-start | bytes 9437192 | tf_op jit(solution)/shard_map/ppermute | solution.py:170
  757.1 171.5 %collective-permute-start.22 = (bf16[1024,2048]{1,0:T(8,128)(2,1)}, bf16[1024,2048]{1,0:T(8,128)(2,1)}, u32[]{:S(2)}, u32[]{:S(2)}) collective-permute-start(bf16[1024,2048]{1,0:T(8,128)(2,1)} %shard_map.48.refs_0_), channel_id=1, source_target_pairs={{0,1},{1,0},{2,3},{3,2},{4,5},{5,4},{6,7},{7,6}} | collective-permute-start | bytes 12582920 | tf_op jit(solution)/shard_map/ppermute | solution.py:170
  848.2 133.0 %collective-permute-start.25 = (bf16[512,4096]{1,0:T(8,128)(2,1)}, bf16[512,4096]{1,0:T(8,128)(2,1)}, u32[]{:S(2)}, u32[]{:S(2)}) collective-permute-start(bf16[512,4096]{1,0:T(8,128)(2,1)} %get-tuple-element.54), channel_id=1, source_target_pairs={{0,2},{1,5},{2,0},{3,7},{4,6},{5,1},{6,4},{7,3}} | collective-permute-start | bytes 12582920 | tf_op jit(solution)/shard_map/ppermute | solution.py:170
  850.0 90.2 %collective-permute-start.24 = (bf16[512,4096]{1,0:T(8,128)(2,1)}, bf16[512,4096]{1,0:T(8,128)(2,1)}, u32[]{:S(2)}, u32[]{:S(2)}) collective-permute-start(bf16[512,4096]{1,0:T(8,128)(2,1)} %get-tuple-element.61), channel_id=1, source_target_pairs={{0,4},{1,3},{2,6},{3,1},{4,0},{5,7},{6,2},{7,5}} | collective-permute-start | bytes 12582920 | tf_op jit(solution)/shard_map/ppermute | solution.py:170
  979.3 41.0 %collective-permute-start.27 = (bf16[512,4096]{1,0:T(8,128)(2,1)}, bf16[512,4096]{1,0:T(8,128)(2,1)}, u32[]{:S(2)}, u32[]{:S(2)}) collective-permute-start(bf16[512,4096]{1,0:T(8,128)(2,1)} %shard_map.60), channel_id=1, source_target_pairs={{0,1},{1,0},{2,3},{3,2},{4,5},{5,4},{6,7},{7,6}} | collective-permute-start | bytes 12582920 | tf_op jit(solution)/shard_map/ppermute | solution.py:170
  979.4 92.8 %collective-permute-start.26 = (bf16[512,4096]{1,0:T(8,128)(2,1)}, bf16[512,4096]{1,0:T(8,128)(2,1)}, u32[]{:S(2)}, u32[]{:S(2)}) collective-permute-start(bf16[512,4096]{1,0:T(8,128)(2,1)} %shard_map.59), channel_id=1, source_target_pairs={{0,4},{1,3},{2,6},{3,1},{4,0},{5,7},{6,2},{7,5}} | collective-permute-start | bytes 12582920 | tf_op jit(solution)/shard_map/ppermute | solution.py:170
  981.0 92.1 %collective-permute-start.28 = (bf16[512,4096]{1,0:T(8,128)(2,1)}, bf16[512,4096]{1,0:T(8,128)(2,1)}, u32[]{:S(2)}, u32[]{:S(2)}) collective-permute-start(bf16[512,4096]{1,0:T(8,128)(2,1)} %shard_map.58), channel_id=1, source_target_pairs={{0,3},{1,4},{2,1},{3,6},{4,7},{5,0},{6,5},{7,2}} | collective-permute-start | bytes 12582920 | tf_op jit(solution)/shard_map/ppermute | solution.py:170

commit v2 on v1

v2 whole, which is shorter than its diff:
```python
import functools

import jax
import jax.numpy as jnp
from jax import lax
from jax.experimental import pallas as pl
from jax.experimental.pallas import tpu as pltpu
from jax.sharding import PartitionSpec as P


BF = jnp.bfloat16
F32 = jnp.float32
VMEM_BYTES = 67_000_000


def mm(a, b):
    return jnp.dot(a, b, preferred_element_type=F32)


def first_step(fn):
    pl.when(pl.program_id(0) == 0)(fn)


def up_tiles(base, x, w, got, xv, wv, xsem, wsem, rv=None, rsem=None):
    i, n = pl.program_id(0), pl.num_programs(0)
    tn = wv.shape[-1]
    slot = lax.rem(i, 2)

    def w_copy(t, j):
        at, cols = lax.rem(t, 2), pl.ds(pl.multiple_of(base + t * tn, tn), tn)
        return pltpu.make_async_copy(w[j].at[:, cols], wv.at[at, j], wsem.at[at, j])

    def r_copy(t, j):
        at, cols = lax.rem(t, 2), pl.ds(pl.multiple_of(t * tn, tn), tn)
        return pltpu.make_async_copy(got[j].at[:, cols], rv.at[at, j], rsem.at[at, j])

    def x_copy(c):
        return pltpu.make_async_copy(x[c], xv.at[c], xsem.at[c])

    @first_step
    def _():
        x_copy(0).start()
        w_copy(0, 0).start()

    w_copy(i, 0).wait()

    @first_step
    def _():
        x_copy(0).wait()
        w_copy(0, 1).start()
        for c in range(1, len(x)):
            x_copy(c).start()
        for j in range(len(got)):
            r_copy(0, j).start()

    first = mm(xv[0], wv[slot, 0])
    w_copy(i, 1).wait()

    @first_step
    def _():
        for c in range(1, len(x)):
            x_copy(c).wait()

    for j in range(len(got)):
        r_copy(i, j).wait()

    @pl.when(i + 1 < n)
    def _():
        for j in range(2):
            w_copy(i + 1, j).start()
        for j in range(len(got)):
            r_copy(i + 1, j).start()

    out = [(first, mm(xv[0], wv[slot, 1]))]
    for c in range(1, len(x)):
        out.append((mm(xv[c], wv[slot, 0]), mm(xv[c], wv[slot, 1])))
    return out


def give_kernel(rows, half, chunks, off, *refs):
    x, (wg, wu, pa, pb), scratch = refs[:chunks], refs[chunks : chunks + 4], refs[chunks + 4 :]
    for c, (a, b) in enumerate(up_tiles(off[0] * half, x, (wg, wu), (), *scratch)):
        pa[pl.ds(c * rows, rows), :] = a.astype(BF)
        pb[pl.ds(c * rows, rows), :] = b.astype(BF)


def keep_kernel(rows, half, chunks, off, *refs):
    x, (wg, wu, ra, rb, h), scratch = refs[:chunks], refs[chunks : chunks + 5], refs[chunks + 5 :]
    rv = scratch[4]
    slot = lax.rem(pl.program_id(0), 2)
    for c, (a, b) in enumerate(up_tiles(off[0] * half, x, (wg, wu), (ra, rb), *scratch)):
        theirs = pl.ds((chunks - 1 - c) * rows, rows)
        a = a + rv[slot, 0, theirs, :].astype(F32)
        b = b + rv[slot, 1, theirs, :].astype(F32)
        h[pl.ds(c * rows, rows), :] = (jax.nn.silu(a) * b).astype(BF)


def down_kernel(rows, half, chunks, n_add, off, own, got, wd, *refs):
    adds, outs = refs[:n_add], refs[n_add : n_add + len(chunks)]
    hv, wv, hsem, wsem = refs[-4:]
    i, n = pl.program_id(0), pl.num_programs(0)
    tn = wv.shape[-1]

    def w_copy(t):
        at, cols = lax.rem(t, 2), pl.ds(pl.multiple_of(t * tn, tn), tn)
        return pltpu.make_async_copy(wd.at[:, cols], wv.at[at], wsem.at[at])

    def h_copies(k):
        for g, (src, c, side) in enumerate(((own, chunks[k][0], off[0]), (got, chunks[k][1], 1 - off[0]))):
            cols = pl.ds(pl.multiple_of(side * half, 128), half)
            yield pltpu.make_async_copy(src.at[pl.ds(c * rows, rows), :], hv.at[k, :, cols], hsem.at[k, g])

    @first_step
    def _():
        for c in h_copies(0):
            c.start()
        w_copy(0).start()

    w_copy(i).wait()

    @first_step
    def _():
        for c in h_copies(0):
            c.wait()
        if len(chunks) > 1:
            for c in h_copies(1):
                c.start()

    @pl.when(i + 1 < n)
    def _():
        w_copy(i + 1).start()

    for k in range(len(chunks)):
        if k:

            @first_step
            def _():
                for c in h_copies(k):
                    c.wait()

        o = mm(hv[k], wv[lax.rem(i, 2)])
        if n_add:
            o = o + adds[k][...].astype(F32)
        outs[k][...] = o.astype(BF)


def finish_kernel(off, x, m0, m1, p0, p1, y):
    n = m0.shape[1]
    for at, lhs, rhs in ((off[0], m0, m1), (1 - off[0], p0, p1)):
        cols = pl.ds(pl.multiple_of(at * n, 128), n)
        o = lhs[...].astype(F32) + rhs[...].astype(F32)
        y[:, cols] = (x[:, cols].astype(F32) + o).astype(BF)


def solution(mesh):
    nt = mesh.shape["tp"]
    nd = mesh.shape["dp"]
    axes = ("tp", "dp")

    def pairs(bit0, bit1, flip):
        return [(t * nd + d, (t ^ (bit0, bit1)[d]) * nd + (d ^ flip)) for t in range(nt) for d in range(nd)]

    perms = {"a": pairs(1, 2, 0), "b": pairs(2, 1, 0), "c": pairs(0, 0, 1), "ax": pairs(1, 2, 1), "bx": pairs(2, 1, 1)}

    def body(x, wg, wu, wd):
        r, d = x.shape
        dc = d // nd
        f = wg.shape[1]
        half, tn = f // 2, 512
        me = lax.axis_index("dp")
        mine, other = me.reshape(1), (1 - me).reshape(1)
        last = [None]
        anywhere = pl.BlockSpec(memory_space=pl.ANY)
        params = pltpu.CompilerParams(dimension_semantics=("arbitrary",), vmem_limit_bytes=VMEM_BYTES)

        def hop(v, kind):
            return lax.ppermute(v, axes, perms[kind])

        def after(v):
            if last[0] is None:
                return v
            return lax.optimization_barrier((v, last[0]))[0]

        def run(call, args):
            out = call(*args)
            last[0] = out[0] if isinstance(out, (list, tuple)) else out
            return out

        def up(kernel, who, xs, got, n_out):
            n = len(xs)
            shape = jax.ShapeDtypeStruct((n * r, half), BF)
            scratch = [
                pltpu.VMEM((n, r, dc), BF),
                pltpu.VMEM((2, 2, dc, tn), BF),
                pltpu.SemaphoreType.DMA((n,)),
                pltpu.SemaphoreType.DMA((2, 2)),
            ]
            if got:
                scratch += [pltpu.VMEM((2, 2, n * r, tn), BF), pltpu.SemaphoreType.DMA((2, 2))]
            call = pl.pallas_call(
                functools.partial(kernel, r, half, n),
                grid_spec=pltpu.PrefetchScalarGridSpec(
                    num_scalar_prefetch=1,
                    grid=(half // tn,),
                    in_specs=[anywhere] * (n + 2 + len(got)),
                    out_specs=[pl.BlockSpec((n * r, tn), lambda i, o: (0, i))] * n_out,
                    scratch_shapes=scratch,
                ),
                out_shape=[shape] * n_out,
                compiler_params=params,
                cost_estimate=pl.CostEstimate(
                    flops=4 * n * r * dc * half, bytes_accessed=4 * (n * r + half) * dc, transcendentals=0
                ),
            )
            return run(call, (who, after(xs[0]), *xs[1:], wg, wu, *got))

        def give(xs):
            pa, pb = up(give_kernel, other, xs, (), 2)
            return hop(pa, "c"), hop(pb, "c")

        def keep(xs, got):
            (h,) = up(keep_kernel, mine, xs, got, 1)
            return h, hop(h, "c")

        def down(own, got, chunks, adds=()):
            n = len(chunks)
            o_spec = pl.BlockSpec((r, tn), lambda i, o: (0, i))
            call = pl.pallas_call(
                functools.partial(down_kernel, r, half, chunks, len(adds)),
                grid_spec=pltpu.PrefetchScalarGridSpec(
                    num_scalar_prefetch=1,
                    grid=(dc // tn,),
                    in_specs=[anywhere] * 3 + [o_spec] * len(adds),
                    out_specs=[o_spec] * n,
                    scratch_shapes=[
                        pltpu.VMEM((n, r, f), BF),
                        pltpu.VMEM((2, f, tn), BF),
                        pltpu.SemaphoreType.DMA((n, 2)),
                        pltpu.SemaphoreType.DMA((2,)),
                    ],
                ),
                out_shape=[jax.ShapeDtypeStruct((r, dc), BF)] * n,
                compiler_params=params,
                cost_estimate=pl.CostEstimate(
                    flops=2 * n * r * f * dc, bytes_accessed=2 * (n * r * f + f * dc + n * r * dc), transcendentals=0
                ),
            )
            return run(call, (mine, after(own), got, wd, *adds))

        xm = lax.dynamic_slice_in_dim(x, me * dc, dc, 1)
        xp = hop(lax.dynamic_slice_in_dim(x, (1 - me) * dc, dc, 1), "c")
        x1m = hop(xm, "a")
        g0m = give((xm,))
        x1p = hop(xp, "b")
        g0p = give((xp,))
        x2m = hop(x1m, "b")
        h0p, t0p = keep((xp,), g0m)
        x2p = hop(x1p, "a")
        u1, u2 = (x1m, x1p), (x2m, x2p)
        g1 = give(u1)
        x3m, x3p = hop(xm, "b"), hop(xp, "a")
        u3 = (x3m, x3p)
        g2 = give(u2)
        h1, t1 = keep(u1, g1)
        h2, t2 = keep(u2, g2)
        g3 = give(u3)
        both = ((0, 1), (1, 0))
        o2m, o2p = down(h2, t2, both)
        s2m, s2p = hop(o2m, "a"), hop(o2p, "b")
        o1m, o1p = down(h1, t1, both)
        y1m, y1p = hop(o1m, "a"), hop(o1p, "b")
        h3, t3 = keep(u3, g3)
        h0m, t0m = keep((xm,), g0p)
        (o3p,) = down(h3, t3, both[1:], (s2p,))
        y3p = hop(o3p, "ax")
        (o3m,) = down(h3, t3, both[:1], (s2m,))
        y3m = hop(o3m, "b")
        (op,) = down(h0p, t0m, ((0, 0),), (y1p,))
        rp = hop(op, "c")
        (om,) = down(h0m, t0p, ((0, 0),), (y1m,))
        rows = min(r, 64)
        half = pl.BlockSpec((rows, dc), lambda i, o: (i, 0))
        full = pl.BlockSpec((rows, d), lambda i, o: (i, 0))
        call = pl.pallas_call(
            finish_kernel,
            grid_spec=pltpu.PrefetchScalarGridSpec(
                num_scalar_prefetch=1, grid=(r // rows,), in_specs=[full] + [half] * 4, out_specs=full
            ),
            out_shape=jax.ShapeDtypeStruct((r, d), BF),
            compiler_params=pltpu.CompilerParams(dimension_semantics=("arbitrary",)),
            cost_estimate=pl.CostEstimate(flops=3 * r * d, bytes_accessed=8 * r * d, transcendentals=0),
            name="finish",
        )
        return run(call, (mine, x, om, y3m, rp, y3p))

    return jax.shard_map(body, mesh=mesh, in_specs=(P(("dp", "tp"), None), P("dp", "tp"), P("dp", "tp"), P("tp", "dp")), out_specs=P(("dp", "tp"), None), check_vma=False)
```

time: 1090 us -> 1070 us (0.982)
  waiting for transfers between devices: 160 us -> 133 us
    ppermute x29, waiting for transfers between devices: 160 us -> 133 us  [hop(): return lax.ppermute(v, axes, perms[kind])]
  transfers between devices with their start and end apart: 29 -> 29, of which waited for: 5 -> 7; matrix products, arithmetic and copies ran while one was open for 0% -> 0% of each run, Pallas kernels for 75% -> 77%
where the time goes in v2:
time: 1070 us; the launch traced here: 1060 us
  Pallas kernels  899 us (84%)
  waiting for transfers between devices  133 us (12%)
  starting transfers between devices  19.9 us (2%)
    pallas_call x17, Pallas kernels, run(): out = call(*args)  899 us
    ppermute x29, waiting for transfers between devices, hop(): return lax.ppermute(v, axes, perms[kind])  133 us
  transfers between devices with their start and end apart: 29, of which 7 were waited for; matrix products, arithmetic and copies ran while one was open for 0% of the time, Pallas kernels for 77%

profile of v2, /device:TPU:0, one launch (start us, length us, event | category | flops | bytes accessed | tf_op | source)
XLA Modules:
  0.0 1060.7 jit_solution(3077098407242018496)
XLA Ops:
  0.0 7.9 constant_dynamic-slice_fusion
  7.9 0.8 collective-permute-start.3
  8.8 37.2 %shard_map.46 = (bf16[512,3584]{1,0:T(8,128)(2,1)}, bf16[512,3584]{1,0:T(8,128)(2,1)}) custom-call(s32[1]{0:T(128)} %bitcast.1.off, bf16[512,4096]{1,0:T(8,128)(2,1)} %get-tuple-element.55.refs_0_, bf16[4096,7168]{1,0:T(8,128)(2,1)} %refs_1_.7, bf16[4096,7168]{1,0:T(8,128)(2,1)} %refs_2_.19), custom_call_target="tpu_custom_call" | custom-call | flops 30064771072 | bytes 67108864 | tf_op jit(solution)/shard_map/pallas_call | solution.py:185
  45.9 0.0 collective-permute-start.4
  46.0 0.5 collective-permute-start.5
  46.5 2.5 collective-permute-start.1
  49.0 0.0 collective-permute-done.3.refs_0_
  49.0 1.5 collective-permute-start.6
  50.5 37.1 %shard_map.47 = (bf16[512,3584]{1,0:T(8,128)(2,1)}, bf16[512,3584]{1,0:T(8,128)(2,1)}) custom-call(s32[1]{0:T(128)} %bitcast.1.off, bf16[512,4096]{1,0:T(8,128)(2,1)} %collective-permute-done.3.refs_0_, bf16[4096,7168]{1,0:T(8,128)(2,1)} %refs_1_.7, bf16[4096,7168]{1,0:T(8,128)(2,1)} %refs_2_.19), custom_call_target="tpu_custom_call" | custom-call | flops 30064771072 | bytes 67108864 | tf_op jit(solution)/shard_map/pallas_call | solution.py:185
  87.7 0.0 collective-permute-done.5.refs_4_
  87.7 42.0 %shard_map.48.own = bf16[512,3584]{1,0:T(8,128)(2,1)} custom-call(s32[1]{0:T(128)} %bitcast.off, bf16[512,4096]{1,0:T(8,128)(2,1)} %collective-permute-done.3.refs_0_, bf16[4096,7168]{1,0:T(8,128)(2,1)} %refs_1_.7, bf16[4096,7168]{1,0:T(8,128)(2,1)} %refs_2_.19, bf16[512,3584]{1,0:T(8,128)(2,1)} %collective-permute-done.4.refs_3_, ...), custom_call_target="tpu_custom_call" | custom-call | flops 30064771072 | bytes 67108864 | tf_op jit(solution)/shard_map/pallas_call | solution.py:185
  129.7 9.8 collective-permute-done.1.refs_0_
  139.5 2.8 collective-permute-start.2
  142.3 1.7 collective-permute-start.7
  144.0 69.2 %shard_map.49 = (bf16[1024,3584]{1,0:T(8,128)(2,1)}, bf16[1024,3584]{1,0:T(8,128)(2,1)}) custom-call(s32[1]{0:T(128)} %bitcast.1.off, bf16[512,4096]{1,0:T(8,128)(2,1)} %collective-permute-done.1.refs_0_, bf16[512,4096]{1,0:T(8,128)(2,1)} %collective-permute-done.6.refs_1_, bf16[4096,7168]{1,0:T(8,128)(2,1)} %refs_1_.7, bf16[4096,7168]{1,0:T(8,128)(2,1)} %refs_2_.19), custom_call_target="tpu_custom_call" | custom-call | flops 60129542144 | bytes 75497472 | tf_op jit(solution)/shard_map/pallas_call | solution.py:185
  213.2 0.0 collective-permute-start.8
  213.3 20.5 %collective-permute-done.2.refs_0_ = bf16[512,4096]{1,0:T(8,128)(2,1)} collective-permute-done((bf16[512,4096]{1,0:T(8,128)(2,1)}, bf16[512,4096]{1,0:T(8,128)(2,1)}, u32[]{:S(2)}, u32[]{:S(2)}) %collective-permute-start.2) | collective-permute-done | bytes 4194336 | tf_op jit(solution)/shard_map/ppermute | solution.py:177
  233.7 0.0 collective-permute-start.9
  233.7 0.0 collective-permute-done.7.refs_1_
  233.7 69.0 %shard_map.50 = (bf16[1024,3584]{1,0:T(8,128)(2,1)}, bf16[1024,3584]{1,0:T(8,128)(2,1)}) custom-call(s32[1]{0:T(128)} %bitcast.1.off, bf16[512,4096]{1,0:T(8,128)(2,1)} %collective-permute-done.2.refs_0_, bf16[512,4096]{1,0:T(8,128)(2,1)} %collective-permute-done.7.refs_1_, bf16[4096,7168]{1,0:T(8,128)(2,1)} %refs_1_.7, bf16[4096,7168]{1,0:T(8,128)(2,1)} %refs_2_.19), custom_call_target="tpu_custom_call" | custom-call | flops 60129542144 | bytes 75497472 | tf_op jit(solution)/shard_map/pallas_call | solution.py:185
  302.7 0.5 collective-permute-start.10
  303.2 0.0 collective-permute-start.11
  303.3 1.6 collective-permute-start
  304.9 0.0 collective-permute-done.8.refs_4_
  304.9 1.3 collective-permute-start.12
  306.2 74.6 %shard_map.51.own = bf16[1024,3584]{1,0:T(8,128)(2,1)} custom-call(s32[1]{0:T(128)} %bitcast.off, bf16[512,4096]{1,0:T(8,128)(2,1)} %collective-permute-done.1.refs_0_, bf16[512,4096]{1,0:T(8,128)(2,1)} %collective-permute-done.6.refs_1_, bf16[4096,7168]{1,0:T(8,128)(2,1)} %refs_1_.7, bf16[4096,7168]{1,0:T(8,128)(2,1)} %refs_2_.19, ...), custom_call_target="tpu_custom_call" | custom-call | flops 60129542144 | bytes 75497472 | tf_op jit(solution)/shard_map/pallas_call | solution.py:185
  380.8 0.0 collective-permute-done.10.refs_4_
  380.8 0.0 collective-permute-done.11.refs_5_
  380.8 74.2 %shard_map.52.own = bf16[1024,3584]{1,0:T(8,128)(2,1)} custom-call(s32[1]{0:T(128)} %bitcast.off, bf16[512,4096]{1,0:T(8,128)(2,1)} %collective-permute-done.2.refs_0_, bf16[512,4096]{1,0:T(8,128)(2,1)} %collective-permute-done.7.refs_1_, bf16[4096,7168]{1,0:T(8,128)(2,1)} %refs_1_.7, bf16[4096,7168]{1,0:T(8,128)(2,1)} %refs_2_.19, ...), custom_call_target="tpu_custom_call" | custom-call | flops 60129542144 | bytes 75497472 | tf_op jit(solution)/shard_map/pallas_call | solution.py:185
  455.0 0.0 collective-permute-start.13
  455.0 0.5 collective-permute-start.14
  455.5 69.3 %shard_map.53 = (bf16[1024,3584]{1,0:T(8,128)(2,1)}, bf16[1024,3584]{1,0:T(8,128)(2,1)}) custom-call(s32[1]{0:T(128)} %bitcast.1.off, bf16[512,4096]{1,0:T(8,128)(2,1)} %collective-permute-done.refs_0_, bf16[512,4096]{1,0:T(8,128)(2,1)} %collective-permute-done.12.refs_1_, bf16[4096,7168]{1,0:T(8,128)(2,1)} %refs_1_.7, bf16[4096,7168]{1,0:T(8,128)(2,1)} %refs_2_.19), custom_call_target="tpu_custom_call" | custom-call | flops 60129542144 | bytes 75497472 | tf_op jit(solution)/shard_map/pallas_call | solution.py:185
  524.8 0.0 collective-permute-start.15
  524.9 0.5 collective-permute-start.16
  525.4 0.0 collective-permute-done.13.got
  525.4 70.7 %shard_map.54 = (bf16[512,4096]{1,0:T(8,128)(2,1)}, bf16[512,4096]{1,0:T(8,128)(2,1)}) custom-call(s32[1]{0:T(128)} %bitcast.off, bf16[1024,3584]{1,0:T(8,128)(2,1)} %shard_map.52.own, bf16[1024,3584]{1,0:T(8,128)(2,1)} %collective-permute-done.13.got, bf16[7168,4096]{1,0:T(8,128)(2,1)} %wd.11), custom_call_target="tpu_custom_call" | custom-call | flops 60129542144 | bytes 81788928 | tf_op jit(solution)/shard_map/pallas_call | solution.py:185
  596.1 0.0 collective-permute-done.14.got
  596.1 70.9 %shard_map.55 = (bf16[512,4096]{1,0:T(8,128)(2,1)}, bf16[512,4096]{1,0:T(8,128)(2,1)}) custom-call(s32[1]{0:T(128)} %bitcast.off, bf16[1024,3584]{1,0:T(8,128)(2,1)} %shard_map.51.own, bf16[1024,3584]{1,0:T(8,128)(2,1)} %collective-permute-done.14.got, bf16[7168,4096]{1,0:T(8,128)(2,1)} %wd.11), custom_call_target="tpu_custom_call" | custom-call | flops 60129542144 | bytes 81788928 | tf_op jit(solution)/shard_map/pallas_call | solution.py:185
  667.0 0.0 collective-permute-done.15.refs_4_
  667.0 74.1 %shard_map.56.own = bf16[1024,3584]{1,0:T(8,128)(2,1)} custom-call(s32[1]{0:T(128)} %bitcast.off, bf16[512,4096]{1,0:T(8,128)(2,1)} %collective-permute-done.refs_0_, bf16[512,4096]{1,0:T(8,128)(2,1)} %collective-permute-done.12.refs_1_, bf16[4096,7168]{1,0:T(8,128)(2,1)} %refs_1_.7, bf16[4096,7168]{1,0:T(8,128)(2,1)} %refs_2_.19, ...), custom_call_target="tpu_custom_call" | custom-call | flops 60129542144 | bytes 75497472 | tf_op jit(solution)/shard_map/pallas_call | solution.py:185
  741.1 0.2 collective-permute-start.19
  741.3 0.3 collective-permute-start.17
  741.7 0.2 collective-permute-start.18
  741.8 0.7 collective-permute-start.20
  742.6 0.1 collective-permute-start.24
  742.6 15.8 %collective-permute-done.17.refs_3_ = bf16[512,3584]{1,0:T(8,128)(2,1)} collective-permute-done((bf16[512,3584]{1,0:T(8,128)(2,1)}, bf16[512,3584]{1,0:T(8,128)(2,1)}, u32[]{:S(2)}, u32[]{:S(2)}) %collective-permute-start.17) | collective-permute-done | bytes 3670048 | tf_op jit(solution)/shard_map/ppermute | solution.py:177
  758.4 0.7 collective-permute-start.21
  759.1 4.5 collective-permute-done.18.refs_4_
  763.7 42.1 %shard_map.57.own = bf16[512,3584]{1,0:T(8,128)(2,1)} custom-call(s32[1]{0:T(128)} %bitcast.off, bf16[512,4096]{1,0:T(8,128)(2,1)} %get-tuple-element.55.refs_0_, bf16[4096,7168]{1,0:T(8,128)(2,1)} %refs_1_.7, bf16[4096,7168]{1,0:T(8,128)(2,1)} %refs_2_.19, bf16[512,3584]{1,0:T(8,128)(2,1)} %collective-permute-done.17.refs_3_, ...), custom_call_target="tpu_custom_call" | custom-call | flops 30064771072 | bytes 67108864 | tf_op jit(solution)/shard_map/pallas_call | solution.py:185
  805.8 0.2 collective-permute-start.22
  806.0 13.8 %collective-permute-done.20.refs_0_ = bf16[512,4096]{1,0:T(8,128)(2,1)} collective-permute-done((bf16[512,4096]{1,0:T(8,128)(2,1)}, bf16[512,4096]{1,0:T(8,128)(2,1)}, u32[]{:S(2)}, u32[]{:S(2)}) %collective-permute-start.20) | collective-permute-done | bytes 4194336 | tf_op jit(solution)/shard_map/ppermute | solution.py:177
  819.8 0.7 collective-permute-start.25
  820.6 0.4 collective-permute-start.23
  821.0 38.9 %shard_map.58 = bf16[512,4096]{1,0:T(8,128)(2,1)} custom-call(s32[1]{0:T(128)} %bitcast.off, bf16[1024,3584]{1,0:T(8,128)(2,1)} %shard_map.56.own, bf16[1024,3584]{1,0:T(8,128)(2,1)} %collective-permute-done.19.got, bf16[7168,4096]{1,0:T(8,128)(2,1)} %wd.11, bf16[512,4096]{1,0:T(8,128)(2,1)} %collective-permute-done.20.refs_0_), custom_call_target="tpu_custom_call" | custom-call | flops 30064771072 | bytes 70254592 | tf_op jit(solution)/shard_map/pallas_call | solution.py:185
  859.9 0.0 collective-permute-done.21.refs_0_
  859.9 38.9 %shard_map.59 = bf16[512,4096]{1,0:T(8,128)(2,1)} custom-call(s32[1]{0:T(128)} %bitcast.off, bf16[1024,3584]{1,0:T(8,128)(2,1)} %shard_map.56.own, bf16[1024,3584]{1,0:T(8,128)(2,1)} %collective-permute-done.19.got, bf16[7168,4096]{1,0:T(8,128)(2,1)} %wd.11, bf16[512,4096]{1,0:T(8,128)(2,1)} %collective-permute-done.21.refs_0_), custom_call_target="tpu_custom_call" | custom-call | flops 30064771072 | bytes 70254592 | tf_op jit(solution)/shard_map/pallas_call | solution.py:185
  898.9 15.4 %collective-permute-done.23.refs_0_ = bf16[512,4096]{1,0:T(8,128)(2,1)} collective-permute-done((bf16[512,4096]{1,0:T(8,128)(2,1)}, bf16[512,4096]{1,0:T(8,128)(2,1)}, u32[]{:S(2)}, u32[]{:S(2)}) %collective-permute-start.23) | collective-permute-done | bytes 4194336 | tf_op jit(solution)/shard_map/ppermute | solution.py:177
  914.3 38.9 %shard_map.60 = bf16[512,4096]{1,0:T(8,128)(2,1)} custom-call(s32[1]{0:T(128)} %bitcast.off, bf16[512,3584]{1,0:T(8,128)(2,1)} %shard_map.48.own, bf16[512,3584]{1,0:T(8,128)(2,1)} %collective-permute-done.22.got, bf16[7168,4096]{1,0:T(8,128)(2,1)} %wd.11, bf16[512,4096]{1,0:T(8,128)(2,1)} %collective-permute-done.23.refs_0_), custom_call_target="tpu_custom_call" | custom-call | flops 30064771072 | bytes 70254592 | tf_op jit(solution)/shard_map/pallas_call | solution.py:185
  953.2 0.0 collective-permute-start.27
  953.3 0.4 collective-permute-start.26
  953.7 1.4 collective-permute-start.28
  955.1 38.9 %shard_map.61.m0 = bf16[512,4096]{1,0:T(8,128)(2,1)} custom-call(s32[1]{0:T(128)} %bitcast.off, bf16[512,3584]{1,0:T(8,128)(2,1)} %shard_map.57.own, bf16[512,3584]{1,0:T(8,128)(2,1)} %collective-permute-done.24.got, bf16[7168,4096]{1,0:T(8,128)(2,1)} %wd.11, bf16[512,4096]{1,0:T(8,128)(2,1)} %collective-permute-done.25.refs_0_), custom_call_target="tpu_custom_call" | custom-call | flops 30064771072 | bytes 70254592 | tf_op jit(solution)/shard_map/pallas_call | solution.py:185
  994.1 52.8 %collective-permute-done.26.m1 = bf16[512,4096]{1,0:T(8,128)(2,1)} collective-permute-done((bf16[512,4096]{1,0:T(8,128)(2,1)}, bf16[512,4096]{1,0:T(8,128)(2,1)}, u32[]{:S(2)}, u32[]{:S(2)}) %collective-permute-start.26) | collective-permute-done | bytes 4194336 | tf_op jit(solution)/shard_map/ppermute | solution.py:177
  1046.9 13.4 %finish.1 = bf16[512,8192]{1,0:T(8,128)(2,1)} custom-call(s32[1]{0:T(128)} %bitcast.off, bf16[512,8192]{1,0:T(8,128)(2,1)} %x.1, bf16[512,4096]{1,0:T(8,128)(2,1)} %shard_map.61.m0, bf16[512,4096]{1,0:T(8,128)(2,1)} %collective-permute-done.26.m1, bf16[512,4096]{1,0:T(8,128)(2,1)} %collective-permute-done.27.p0, bf16[512,4096]{1,0:T(8,128)(2,1)} %collective-permute-done.28.p1), custom_call_target="tpu_custom_call" | custom-call | flops 12582912 | bytes 33554432 | tf_op jit(solution)/shard_map/finish/pallas_call | solution.py:185
  (12 shorter events, 0.0 us)
Async XLA Ops:
  7.9 41.1 %collective-permute-start.3 = (bf16[512,4096]{1,0:T(8,128)(2,1)}, bf16[512,4096]{1,0:T(8,128)(2,1)}, u32[]{:S(2)}, u32[]{:S(2)}) collective-permute-start(bf16[512,4096]{1,0:T(8,128)(2,1)} %get-tuple-element.63), channel_id=1, source_target_pairs={{0,1},{1,0},{2,3},{3,2},{4,5},{5,4},{6,7},{7,6}} | collective-permute-start | bytes 12582920 | tf_op jit(solution)/shard_map/ppermute | solution.py:177
  45.9 41.7 %collective-permute-start.4 = (bf16[512,3584]{1,0:T(8,128)(2,1)}, bf16[512,3584]{1,0:T(8,128)(2,1)}, u32[]{:S(2)}, u32[]{:S(2)}) collective-permute-start(bf16[512,3584]{1,0:T(8,128)(2,1)} %get-tuple-element.34), channel_id=1, source_target_pairs={{0,1},{1,0},{2,3},{3,2},{4,5},{5,4},{6,7},{7,6}} | collective-permute-start | bytes 11010056 | tf_op jit(solution)/shard_map/ppermute | solution.py:177
  46.0 41.7 %collective-permute-start.5 = (bf16[512,3584]{1,0:T(8,128)(2,1)}, bf16[512,3584]{1,0:T(8,128)(2,1)}, u32[]{:S(2)}, u32[]{:S(2)}) collective-permute-start(bf16[512,3584]{1,0:T(8,128)(2,1)} %get-tuple-element.38), channel_id=1, source_target_pairs={{0,1},{1,0},{2,3},{3,2},{4,5},{5,4},{6,7},{7,6}} | collective-permute-start | bytes 11010056 | tf_op jit(solution)/shard_map/ppermute | solution.py:177
  46.5 93.0 %collective-permute-start.1 = (bf16[512,4096]{1,0:T(8,128)(2,1)}, bf16[512,4096]{1,0:T(8,128)(2,1)}, u32[]{:S(2)}, u32[]{:S(2)}) collective-permute-start(bf16[512,4096]{1,0:T(8,128)(2,1)} %get-tuple-element.55.refs_0_), channel_id=1, source_target_pairs={{0,2},{1,5},{2,0},{3,7},{4,6},{5,1},{6,4},{7,3}} | collective-permute-start | bytes 12582920 | tf_op jit(solution)/shard_map/ppermute | solution.py:177
  49.0 93.3 %collective-permute-start.6 = (bf16[512,4096]{1,0:T(8,128)(2,1)}, bf16[512,4096]{1,0:T(8,128)(2,1)}, u32[]{:S(2)}, u32[]{:S(2)}) collective-permute-start(bf16[512,4096]{1,0:T(8,128)(2,1)} %collective-permute-done.3.refs_0_), channel_id=1, source_target_pairs={{0,4},{1,3},{2,6},{3,1},{4,0},{5,7},{6,2},{7,5}} | collective-permute-start | bytes 12582920 | tf_op jit(solution)/shard_map/ppermute | solution.py:177
  139.5 94.2 %collective-permute-start.2 = (bf16[512,4096]{1,0:T(8,128)(2,1)}, bf16[512,4096]{1,0:T(8,128)(2,1)}, u32[]{:S(2)}, u32[]{:S(2)}) collective-permute-start(bf16[512,4096]{1,0:T(8,128)(2,1)} %collective-permute-done.1.refs_0_), channel_id=1, source_target_pairs={{0,4},{1,3},{2,6},{3,1},{4,0},{5,7},{6,2},{7,5}} | collective-permute-start | bytes 12582920 | tf_op jit(solution)/shard_map/ppermute | solution.py:177
  142.3 91.4 %collective-permute-start.7 = (bf16[512,4096]{1,0:T(8,128)(2,1)}, bf16[512,4096]{1,0:T(8,128)(2,1)}, u32[]{:S(2)}, u32[]{:S(2)}) collective-permute-start(bf16[512,4096]{1,0:T(8,128)(2,1)} %collective-permute-done.6.refs_1_), channel_id=1, source_target_pairs={{0,2},{1,5},{2,0},{3,7},{4,6},{5,1},{6,4},{7,3}} | collective-permute-start | bytes 12582920 | tf_op jit(solution)/shard_map/ppermute | solution.py:177
  213.2 91.7 %collective-permute-start.8 = (bf16[1024,3584]{1,0:T(8,128)(2,1)}, bf16[1024,3584]{1,0:T(8,128)(2,1)}, u32[]{:S(2)}, u32[]{:S(2)}) collective-permute-start(bf16[1024,3584]{1,0:T(8,128)(2,1)} %get-tuple-element.40), channel_id=1, source_target_pairs={{0,1},{1,0},{2,3},{3,2},{4,5},{5,4},{6,7},{7,6}} | collective-permute-start | bytes 22020104 | tf_op jit(solution)/shard_map/ppermute | solution.py:177
  233.7 72.5 %collective-permute-start.9 = (bf16[1024,3584]{1,0:T(8,128)(2,1)}, bf16[1024,3584]{1,0:T(8,128)(2,1)}, u32[]{:S(2)}, u32[]{:S(2)}) collective-permute-start(bf16[1024,3584]{1,0:T(8,128)(2,1)} %get-tuple-element.44), channel_id=1, source_target_pairs={{0,1},{1,0},{2,3},{3,2},{4,5},{5,4},{6,7},{7,6}} | collective-permute-start | bytes 22020104 | tf_op jit(solution)/shard_map/ppermute | solution.py:177
  302.7 78.1 %collective-permute-start.10 = (bf16[1024,3584]{1,0:T(8,128)(2,1)}, bf16[1024,3584]{1,0:T(8,128)(2,1)}, u32[]{:S(2)}, u32[]{:S(2)}) collective-permute-start(bf16[1024,3584]{1,0:T(8,128)(2,1)} %get-tuple-element.42), channel_id=1, source_target_pairs={{0,1},{1,0},{2,3},{3,2},{4,5},{5,4},{6,7},{7,6}} | collective-permute-start | bytes 22020104 | tf_op jit(solution)/shard_map/ppermute | solution.py:177
  303.2 77.5 %collective-permute-start.11 = (bf16[1024,3584]{1,0:T(8,128)(2,1)}, bf16[1024,3584]{1,0:T(8,128)(2,1)}, u32[]{:S(2)}, u32[]{:S(2)}) collective-permute-start(bf16[1024,3584]{1,0:T(8,128)(2,1)} %get-tuple-element.46), channel_id=1, source_target_pairs={{0,1},{1,0},{2,3},{3,2},{4,5},{5,4},{6,7},{7,6}} | collective-permute-start | bytes 22020104 | tf_op jit(solution)/shard_map/ppermute | solution.py:177
  303.3 152.2 %collective-permute-start = (bf16[512,4096]{1,0:T(8,128)(2,1)}, bf16[512,4096]{1,0:T(8,128)(2,1)}, u32[]{:S(2)}, u32[]{:S(2)}) collective-permute-start(bf16[512,4096]{1,0:T(8,128)(2,1)} %get-tuple-element.55.refs_0_), channel_id=1, source_target_pairs={{0,4},{1,3},{2,6},{3,1},{4,0},{5,7},{6,2},{7,5}} | collective-permute-start | bytes 12582920 | tf_op jit(solution)/shard_map/ppermute | solution.py:177
  304.9 150.6 %collective-permute-start.12 = (bf16[512,4096]{1,0:T(8,128)(2,1)}, bf16[512,4096]{1,0:T(8,128)(2,1)}, u32[]{:S(2)}, u32[]{:S(2)}) collective-permute-start(bf16[512,4096]{1,0:T(8,128)(2,1)} %collective-permute-done.3.refs_0_), channel_id=1, source_target_pairs={{0,2},{1,5},{2,0},{3,7},{4,6},{5,1},{6,4},{7,3}} | collective-permute-start | bytes 12582920 | tf_op jit(solution)/shard_map/ppermute | solution.py:177
  455.0 70.4 %collective-permute-start.13 = (bf16[1024,3584]{1,0:T(8,128)(2,1)}, bf16[1024,3584]{1,0:T(8,128)(2,1)}, u32[]{:S(2)}, u32[]{:S(2)}) collective-permute-start(bf16[1024,3584]{1,0:T(8,128)(2,1)} %shard_map.52.own), channel_id=1, source_target_pairs={{0,1},{1,0},{2,3},{3,2},{4,5},{5,4},{6,7},{7,6}} | collective-permute-start | bytes 22020104 | tf_op jit(solution)/shard_map/ppermute | solution.py:177
  455.0 141.0 %collective-permute-start.14 = (bf16[1024,3584]{1,0:T(8,128)(2,1)}, bf16[1024,3584]{1,0:T(8,128)(2,1)}, u32[]{:S(2)}, u32[]{:S(2)}) collective-permute-start(bf16[1024,3584]{1,0:T(8,128)(2,1)} %shard_map.51.own), channel_id=1, source_target_pairs={{0,1},{1,0},{2,3},{3,2},{4,5},{5,4},{6,7},{7,6}} | collective-permute-start | bytes 22020104 | tf_op jit(solution)/shard_map/ppermute | solution.py:177
  524.8 142.1 %collective-permute-start.15 = (bf16[1024,3584]{1,0:T(8,128)(2,1)}, bf16[1024,3584]{1,0:T(8,128)(2,1)}, u32[]{:S(2)}, u32[]{:S(2)}) collective-permute-start(bf16[1024,3584]{1,0:T(8,128)(2,1)} %get-tuple-element.48), channel_id=1, source_target_pairs={{0,1},{1,0},{2,3},{3,2},{4,5},{5,4},{6,7},{7,6}} | collective-permute-start | bytes 22020104 | tf_op jit(solution)/shard_map/ppermute | solution.py:177
  524.9 142.1 %collective-permute-start.16 = (bf16[1024,3584]{1,0:T(8,128)(2,1)}, bf16[1024,3584]{1,0:T(8,128)(2,1)}, u32[]{:S(2)}, u32[]{:S(2)}) collective-permute-start(bf16[1024,3584]{1,0:T(8,128)(2,1)} %get-tuple-element.54), channel_id=1, source_target_pairs={{0,1},{1,0},{2,3},{3,2},{4,5},{5,4},{6,7},{7,6}} | collective-permute-start | bytes 22020104 | tf_op jit(solution)/shard_map/ppermute | solution.py:177
  741.1 79.4 %collective-permute-start.19 = (bf16[1024,3584]{1,0:T(8,128)(2,1)}, bf16[1024,3584]{1,0:T(8,128)(2,1)}, u32[]{:S(2)}, u32[]{:S(2)}) collective-permute-start(bf16[1024,3584]{1,0:T(8,128)(2,1)} %shard_map.56.own), channel_id=1, source_target_pairs={{0,1},{1,0},{2,3},{3,2},{4,5},{5,4},{6,7},{7,6}} | collective-permute-start | bytes 22020104 | tf_op jit(solution)/shard_map/ppermute | solution.py:177
  741.3 17.1 %collective-permute-start.17 = (bf16[512,3584]{1,0:T(8,128)(2,1)}, bf16[512,3584]{1,0:T(8,128)(2,1)}, u32[]{:S(2)}, u32[]{:S(2)}) collective-permute-start(bf16[512,3584]{1,0:T(8,128)(2,1)} %get-tuple-element.36), channel_id=1, source_target_pairs={{0,1},{1,0},{2,3},{3,2},{4,5},{5,4},{6,7},{7,6}} | collective-permute-start | bytes 11010056 | tf_op jit(solution)/shard_map/ppermute | solution.py:177
  741.7 22.0 %collective-permute-start.18 = (bf16[512,3584]{1,0:T(8,128)(2,1)}, bf16[512,3584]{1,0:T(8,128)(2,1)}, u32[]{:S(2)}, u32[]{:S(2)}) collective-permute-start(bf16[512,3584]{1,0:T(8,128)(2,1)} %get-tuple-element.56), channel_id=1, source_target_pairs={{0,1},{1,0},{2,3},{3,2},{4,5},{5,4},{6,7},{7,6}} | collective-permute-start | bytes 11010056 | tf_op jit(solution)/shard_map/ppermute | solution.py:177
  741.8 78.0 %collective-permute-start.20 = (bf16[512,4096]{1,0:T(8,128)(2,1)}, bf16[512,4096]{1,0:T(8,128)(2,1)}, u32[]{:S(2)}, u32[]{:S(2)}) collective-permute-start(bf16[512,4096]{1,0:T(8,128)(2,1)} %get-tuple-element.58), channel_id=1, source_target_pairs={{0,4},{1,3},{2,6},{3,1},{4,0},{5,7},{6,2},{7,5}} | collective-permute-start | bytes 12582920 | tf_op jit(solution)/shard_map/ppermute | solution.py:177
  742.6 212.5 %collective-permute-start.24 = (bf16[512,3584]{1,0:T(8,128)(2,1)}, bf16[512,3584]{1,0:T(8,128)(2,1)}, u32[]{:S(2)}, u32[]{:S(2)}) collective-permute-start(bf16[512,3584]{1,0:T(8,128)(2,1)} %shard_map.48.own), channel_id=1, source_target_pairs={{0,1},{1,0},{2,3},{3,2},{4,5},{5,4},{6,7},{7,6}} | collective-permute-start | bytes 11010056 | tf_op jit(solution)/shard_map/ppermute | solution.py:177
  758.4 101.5 %collective-permute-start.21 = (bf16[512,4096]{1,0:T(8,128)(2,1)}, bf16[512,4096]{1,0:T(8,128)(2,1)}, u32[]{:S(2)}, u32[]{:S(2)}) collective-permute-start(bf16[512,4096]{1,0:T(8,128)(2,1)} %get-tuple-element.50), channel_id=1, source_target_pairs={{0,2},{1,5},{2,0},{3,7},{4,6},{5,1},{6,4},{7,3}} | collective-permute-start | bytes 12582920 | tf_op jit(solution)/shard_map/ppermute | solution.py:177
  805.8 93.1 %collective-permute-start.22 = (bf16[512,3584]{1,0:T(8,128)(2,1)}, bf16[512,3584]{1,0:T(8,128)(2,1)}, u32[]{:S(2)}, u32[]{:S(2)}) collective-permute-start(bf16[512,3584]{1,0:T(8,128)(2,1)} %shard_map.57.own), channel_id=1, source_target_pairs={{0,1},{1,0},{2,3},{3,2},{4,5},{5,4},{6,7},{7,6}} | collective-permute-start | bytes 11010056 | tf_op jit(solution)/shard_map/ppermute | solution.py:177
  819.8 135.3 %collective-permute-start.25 = (bf16[512,4096]{1,0:T(8,128)(2,1)}, bf16[512,4096]{1,0:T(8,128)(2,1)}, u32[]{:S(2)}, u32[]{:S(2)}) collective-permute-start(bf16[512,4096]{1,0:T(8,128)(2,1)} %get-tuple-element.52), channel_id=1, source_target_pairs={{0,2},{1,5},{2,0},{3,7},{4,6},{5,1},{6,4},{7,3}} | collective-permute-start | bytes 12582920 | tf_op jit(solution)/shard_map/ppermute | solution.py:177
  820.6 93.8 %collective-permute-start.23 = (bf16[512,4096]{1,0:T(8,128)(2,1)}, bf16[512,4096]{1,0:T(8,128)(2,1)}, u32[]{:S(2)}, u32[]{:S(2)}) collective-permute-start(bf16[512,4096]{1,0:T(8,128)(2,1)} %get-tuple-element.61), channel_id=1, source_target_pairs={{0,4},{1,3},{2,6},{3,1},{4,0},{5,7},{6,2},{7,5}} | collective-permute-start | bytes 12582920 | tf_op jit(solution)/shard_map/ppermute | solution.py:177
  953.2 40.8 %collective-permute-start.27 = (bf16[512,4096]{1,0:T(8,128)(2,1)}, bf16[512,4096]{1,0:T(8,128)(2,1)}, u32[]{:S(2)}, u32[]{:S(2)}) collective-permute-start(bf16[512,4096]{1,0:T(8,128)(2,1)} %shard_map.60), channel_id=1, source_target_pairs={{0,1},{1,0},{2,3},{3,2},{4,5},{5,4},{6,7},{7,6}} | collective-permute-start | bytes 12582920 | tf_op jit(solution)/shard_map/ppermute | solution.py:177
  953.3 93.6 %collective-permute-start.26 = (bf16[512,4096]{1,0:T(8,128)(2,1)}, bf16[512,4096]{1,0:T(8,128)(2,1)}, u32[]{:S(2)}, u32[]{:S(2)}) collective-permute-start(bf16[512,4096]{1,0:T(8,128)(2,1)} %shard_map.59), channel_id=1, source_target_pairs={{0,4},{1,3},{2,6},{3,1},{4,0},{5,7},{6,2},{7,5}} | collective-permute-start | bytes 12582920 | tf_op jit(solution)/shard_map/ppermute | solution.py:177
  953.7 93.2 %collective-permute-start.28 = (bf16[512,4096]{1,0:T(8,128)(2,1)}, bf16[512,4096]{1,0:T(8,128)(2,1)}, u32[]{:S(2)}, u32[]{:S(2)}) collective-permute-start(bf16[512,4096]{1,0:T(8,128)(2,1)} %shard_map.58), channel_id=1, source_target_pairs={{0,3},{1,4},{2,1},{3,6},{4,7},{5,0},{6,5},{7,2}} | collective-permute-start | bytes 12582920 | tf_op jit(solution)/shard_map/ppermute | solution.py:177
